TPU v7x, 32 devices: a whole 2x2x4 slice. The times are simulated.
32 devices in a mesh: dp: 2 (over x), row: 4 (over z), col: 4 (over y, core).
Axes of the slice: x: 2, y: 2, z: 4, core: 2. Of those that a mesh axis runs over, the one named last changes fastest.
Arguments:
- pair_rep: bfloat16 [1024, 512, 128], P(('dp', 'row'), 'col'), parts along dimension 0
- res_mask: int32 [1024], P('dp'), parts along dimension 0
- ln_gamma: float32 [128], replicated
- ln_beta: float32 [128], replicated
- w_q: bfloat16 [128, 128], replicated
- w_k: bfloat16 [128, 128], replicated
- w_v: bfloat16 [128, 128], replicated
- w_b: bfloat16 [128, 4], replicated
- w_g: bfloat16 [128, 128], replicated
- w_o: bfloat16 [128, 128], replicated
Outputs:
- output: bfloat16 [1024, 512, 128], P(('dp', 'row'), 'col'), parts along dimension 0
There are 2 independent parts. A program takes and returns all parts, laid end to end along the dimension named above; an argument that names none is the same for every part.
All inputs are finite; a program needn't handle non-finite values.
Results may differ from a plain program's by a relative error of at most 0.00749931.
Values are sent between devices in bfloat16 or wider.
A program may use at most 1 GiB of HBM per device.

v0:
```python
import jax
import jax.numpy as jnp
from jax import lax
from jax.sharding import PartitionSpec as P, NamedSharding

LN_EPS = 1e-5


def layer_norm(pair_rep, ln_gamma, ln_beta):
    pair_f32 = pair_rep.astype(jnp.float32)
    mean_c = jnp.mean(pair_f32, axis=-1, keepdims=True)
    centered = pair_f32 - mean_c
    var_c = jnp.mean(jnp.square(centered), axis=-1, keepdims=True)
    return (centered * lax.rsqrt(var_c + LN_EPS) * ln_gamma + ln_beta).astype(jnp.bfloat16)


def solution(mesh):
    col_size = mesh.shape['col']
    shift_pairs = [(src_dev, (src_dev + 1) % col_size) for src_dev in range(col_size)]
    tile_spec = P(('dp', 'row'), 'col', None)

    def per_device(pair_tile, res_mask, ln_gamma, ln_beta, w_q, w_k, w_v, w_b, w_g, w_o):
        row_len, col_len, chan_dim = pair_tile.shape
        num_heads = w_b.shape[1]
        head_dim = w_q.shape[1] // num_heads
        col_idx = lax.axis_index('col')
        normed = layer_norm(pair_tile, ln_gamma, ln_beta)
        head_shape = (row_len, col_len, num_heads, head_dim)
        queries = (jnp.dot(normed, w_q, preferred_element_type=jnp.float32) * head_dim ** -0.5).astype(jnp.bfloat16).reshape(head_shape)
        key_blk = jnp.dot(normed, w_k, preferred_element_type=jnp.float32).astype(jnp.bfloat16).reshape(head_shape)
        val_blk = jnp.dot(normed, w_v, preferred_element_type=jnp.float32).astype(jnp.bfloat16).reshape(head_shape)
        gate_vals = jax.nn.sigmoid(jnp.dot(normed, w_g, preferred_element_type=jnp.float32))
        bias_tile = jnp.dot(normed, w_b, preferred_element_type=jnp.float32).astype(jnp.bfloat16)
        bias_cols = lax.all_gather(bias_tile, 'row', axis=0, tiled=True)
        bias_rows = lax.all_to_all(bias_cols, 'col', 0, 1, tiled=True)
        key_bias = jnp.where(res_mask > 0, 0.0, -1e9).astype(jnp.float32)
        full_bias = jnp.transpose(bias_rows, (2, 0, 1)).astype(jnp.float32) + key_bias

        def fold_block(fold_state, key_part, val_part, src_col):
            run_max, run_sum, acc_out = fold_state
            bias_part = lax.dynamic_slice_in_dim(full_bias, src_col * col_len, col_len, axis=2)
            logits = jnp.einsum('ijhd,ikhd->ihjk', queries, key_part, preferred_element_type=jnp.float32) + bias_part
            new_max = jnp.maximum(run_max, jnp.max(logits, axis=-1))
            rescale = jnp.exp(run_max - new_max)
            weights = jnp.exp(logits - new_max[..., None])
            run_sum = run_sum * rescale + jnp.sum(weights, axis=-1)
            acc_out = acc_out * rescale[..., None] + jnp.einsum('ihjk,ikhd->ihjd', weights.astype(jnp.bfloat16), val_part, preferred_element_type=jnp.float32)
            return new_max, run_sum, acc_out

        stat_shape = (row_len, num_heads, col_len)
        init_state = (jnp.full(stat_shape, -jnp.inf, jnp.float32), jnp.zeros(stat_shape, jnp.float32), jnp.zeros(stat_shape + (head_dim,), jnp.float32))
        first_state = fold_block(init_state, key_blk, val_blk, col_idx)

        def hop_step(hop_idx, loop_state):
            kv_blocks, fold_state = loop_state
            kv_blocks = lax.ppermute(kv_blocks, 'col', shift_pairs)
            src_col = (col_idx + col_size - hop_idx) % col_size
            return kv_blocks, fold_block(fold_state, kv_blocks[0], kv_blocks[1], src_col)

        final_state = lax.fori_loop(1, col_size, hop_step, ((key_blk, val_blk), first_state))
        run_sum = final_state[1][1]
        acc_out = final_state[1][2]
        attended = jnp.transpose(acc_out / run_sum[..., None], (0, 2, 1, 3)).reshape(row_len, col_len, num_heads * head_dim)
        gated_out = (gate_vals * attended).astype(jnp.bfloat16)
        update = jnp.dot(gated_out, w_o, preferred_element_type=jnp.float32)
        return (pair_tile.astype(jnp.float32) + update).astype(jnp.bfloat16)

    return jax.shard_map(per_device, mesh=mesh, in_specs=(tile_spec, P('dp'), P(), P(), P(), P(), P(), P(), P(), P()), out_specs=tile_spec, check_vma=False)
```

profile of v0, /device:TPU:0, one launch (start us, length us, event | category | flops | bytes accessed | tf_op | source)
XLA Modules:
  0.0 488.2 jit_solution(16413768378487128486)
XLA Ops:
  3.6 6.0 %fusion.16 = f32[128,128]{1,0:T(8,128)S(1)} fusion(bf16[128,128,128]{2,1,0:T(8,128)(2,1)} %param.12, f32[128,128]{1,0:T(8,128)S(1)} %broadcast_multiply_fusion), kind=kLoop, calls=%fused_computation.23 | loop fusion | flops 8372224 | bytes 4325376 | tf_op jit(solution)/shard_map/reduce_sum | solution.py:13
  9.7 5.8 %convolution_convert_fusion.2 = bf16[128,128,4]{1,2,0:T(4,128)(2,1)S(1)} fusion(bf16[128,4]{0,1:T(4,128)(2,1)S(1)} %copy-done.14, bf16[128,128,128]{2,1,0:T(8,128)(2,1)S(1)} %copy-done.3, f32[128]{0:T(128)S(1)} %copy-done.15, f32[128]{0:T(128)S(1)} %copy-done.17, f32[128,128]{1,0:T(8,128)S(1)} %add_rsqrt_fusion, f32[128,128]{1,0:T(8,128)S(1)} %broadcast_multiply_fusion), kind=kOutput, calls=%fused_computation.36 | convolution fusion | flops 29425664 | bytes 4458496 | tf_op jit(solution)/shard_map/dot_general | solution.py:33
  15.5 17.5 %all_gather.3 = bf16[512,128,4]{1,2,0:T(4,128)(2,1)} all-gather(bf16[128,128,4]{1,2,0:T(4,128)(2,1)S(1)} %convolution_convert_fusion.2), channel_id=1, replica_groups=mesh['dp'=2,'row'=4,'col'=4] {'row'}, dimensions={0}, use_global_device_ids=true | all-gather | bytes 655360 | tf_op jit(solution)/shard_map/all_gather | solution.py:34
  36.8 8.2 %multiply_convert_fusion.1 = bf16[128,128,128]{1,2,0:T(8,128)(2,1)} fusion(bf16[128,128]{1,0:T(8,128)(2,1)S(1)} %copy-done, bf16[128,128,128]{2,1,0:T(8,128)(2,1)} %param.12, f32[128]{0:T(128)S(1)} %copy-done.15, f32[128]{0:T(128)S(1)} %copy-done.17, f32[128,128]{1,0:T(8,128)S(1)} %add_rsqrt_fusion, f32[128,128]{1,0:T(8,128)S(1)} %broadcast_multiply_fusion), kind=kOutput, calls=%fused_computation.29 | convolution fusion | flops 553648128 | bytes 8553472 | tf_op jit(solution)/shard_map/dot_general | solution.py:29
  44.9 7.5 %convolution_convert_fusion.1 = bf16[128,128,128]{1,2,0:T(8,128)(2,1)} fusion(bf16[128,128]{1,0:T(8,128)(2,1)S(1)} %copy-done.10, bf16[128,128,128]{2,1,0:T(8,128)(2,1)S(1)} %copy-done.4, f32[128]{0:T(128)S(1)} %copy-done.15, f32[128]{0:T(128)S(1)} %copy-done.17, f32[128,128]{1,0:T(8,128)S(1)} %add_rsqrt_fusion, f32[128,128]{1,0:T(8,128)S(1)} %broadcast_multiply_fusion), kind=kOutput, calls=%fused_computation.35 | convolution fusion | flops 551550976 | bytes 8553472 | tf_op jit(solution)/shard_map/dot_general | solution.py:30
  52.4 8.0 %convolution_convert_fusion = bf16[128,128,128]{1,2,0:T(8,128)(2,1)} fusion(bf16[128,128]{1,0:T(8,128)(2,1)S(1)} %copy-done.11, bf16[128,128,128]{2,1,0:T(8,128)(2,1)} %param.12, f32[128]{0:T(128)S(1)} %copy-done.15, f32[128]{0:T(128)S(1)} %copy-done.17, f32[128,128]{1,0:T(8,128)S(1)} %add_rsqrt_fusion, f32[128,128]{1,0:T(8,128)S(1)} %broadcast_multiply_fusion), kind=kOutput, calls=%fused_computation.34 | convolution fusion | flops 551550976 | bytes 8553472 | tf_op jit(solution)/shard_map/dot_general | solution.py:31
  61.0 15.9 %add_reduce_fusion.1 = (f32[128,4,128]{2,1,0:T(4,128)S(1)}, f32[128,4,128,128]{2,3,1,0:T(8,128)}) fusion(f32[4,128,128]{1,2,0:T(8,128)S(1)} %dynamic-slice_bitcast_fusion, bf16[128,128,4,32]{1,3,2,0:T(8,128)(2,1)} %bitcast.66, bf16[128,128,4,32]{1,3,2,0:T(8,128)(2,1)} %bitcast.75), kind=kOutput, calls=%fused_computation.12 | convolution fusion | flops 553582592 | bytes 42467328 | tf_op jit(solution)/shard_map/ijhd,ikhd->ihjk/dot_general | solution.py:42
  77.0 14.8 %fusion.9 = f32[128,4,128]{2,1,0:T(4,128)S(1)} fusion(f32[128,4,128,128]{2,3,1,0:T(8,128)} %get-tuple-element.256, f32[128,4,128]{2,1,0:T(4,128)S(1)} %get-tuple-element.327, f32[4,128,128]{1,2,0:T(8,128)S(1)} %dynamic-slice_bitcast_fusion), kind=kLoop, calls=%fused_computation.14 | loop fusion | flops 25100288 | bytes 34340864 | tf_op jit(solution)/shard_map/reduce_sum | solution.py:46
  92.0 18.3 %broadcast_add_fusion = f32[128,4,128,32]{2,3,1,0:T(8,128)} fusion(f32[128,4,128]{2,1,0:T(4,128)S(1)} %get-tuple-element.253, bf16[128,128,4,32]{1,3,2,0:T(8,128)(2,1)} %bitcast.73, f32[128,4,128,128]{2,3,1,0:T(8,128)} %get-tuple-element.256, f32[128,4,128]{2,1,0:T(4,128)S(1)} %get-tuple-element.327, f32[4,128,128]{1,2,0:T(8,128)S(1)} %dynamic-slice_bitcast_fusion), kind=kOutput, calls=%fused_computation.31 | convolution fusion | flops 564133888 | bytes 46923776 | tf_op jit(solution)/shard_map/ihjk,ikhd->ihjd/dot_general | solution.py:47
  110.3 349.6 %while.23 = (s32[]{:T(128)}, bf16[128,128,4,32]{1,3,2,0:T(8,128)(2,1)}, bf16[128,128,4,32]{1,3,2,0:T(8,128)(2,1)}, f32[128,4,128]{2,1,0:T(4,128)S(1)}, f32[128,4...) while((s32[]{:T(128)}, ...), condition=%wide.region_7.8_spmd, body=%wide.region_4.7_spmd.sunk | while | flops 1145176064 | bytes 244580848 | solution.py:60
  112.2 46.0 %collective-permute-done = bf16[128,128,4,32]{1,3,2,0:T(8,128)(2,1)} collective-permute-done((bf16[128,128,4,32]{1,3,2,0:T(8,128)(2,1)}, bf16[128,128,4,32]{1,3,2,0:T(8,128)(2,1)}, u32[]{:S(2)}, u32[]{:S(2)}) %collective-permute-start) | collective-permute-done | bytes 4194336 | tf_op jit(solution)/shard_map/while/body/eval_jaxpr/ppermute | solution.py:56
  158.2 15.9 %add_reduce_fusion.3 = (f32[128,4,128]{2,1,0:T(4,128)S(1)}, f32[128,4,128,128]{2,3,1,0:T(8,128)}) fusion(f32[4,128,128]{1,2,0:T(8,128)S(1)} %constant_dynamic-slice_fusion.2, bf16[128,128,4,32]{1,3,2,0:T(8,128)(2,1)} %get-tuple-element.360, bf16[128,128,4,32]{1,3,2,0:T(8,128)(2,1)} %collective-permute-done), kind=kOutput, calls=%fused_computation.1.clone.1 | convolution fusion | flops 553582592 | bytes 42467328 | tf_op jit(solution)/shard_map/while/body/eval_jaxpr/ijhd,ikhd->ihjk/dot_general | solution.py:42
  174.2 14.8 %fusion.56 = f32[128,4,128]{2,1,0:T(4,128)S(1)} fusion(f32[128,4,128,128]{2,3,1,0:T(8,128)} %get-tuple-element.321, f32[128,4,128]{2,1,0:T(4,128)S(1)} %max.11, f32[4,128,128]{1,2,0:T(8,128)S(1)} %constant_dynamic-slice_fusion.2), kind=kLoop, calls=%fused_computation.3.clone.1 | loop fusion | flops 25100288 | bytes 34340864 | tf_op jit(solution)/shard_map/while/body/eval_jaxpr/reduce_sum | solution.py:46
  189.3 5.9 %copy.46 = bf16[128,128,4,32]{1,3,2,0:T(8,128)(2,1)} copy(bf16[128,128,4,32]{1,3,2,0:T(8,128)(2,1)} %collective-permute-done) | data formatting | bytes 8388608 | tf_op jit(solution)/shard_map/while
  195.2 7.9 %collective-permute-done.1 = bf16[128,128,4,32]{1,3,2,0:T(8,128)(2,1)} collective-permute-done((bf16[128,128,4,32]{1,3,2,0:T(8,128)(2,1)}, bf16[128,128,4,32]{1,3,2,0:T(8,128)(2,1)}, u32[]{:S(2)}, u32[]{:S(2)}) %collective-permute-start.1) | collective-permute-done | bytes 4194336 | tf_op jit(solution)/shard_map/while/body/eval_jaxpr/ppermute | solution.py:56
  203.2 5.7 %copy.47 = bf16[128,128,4,32]{1,3,2,0:T(8,128)(2,1)} copy(bf16[128,128,4,32]{1,3,2,0:T(8,128)(2,1)} %collective-permute-done.1) | data formatting | bytes 8388608 | tf_op jit(solution)/shard_map/while
  208.9 14.8 %multiply_add_fusion.5 = f32[128,4,128,32]{2,3,1,0:T(8,128)S(1)} fusion(f32[128,4,128,32]{2,3,1,0:T(8,128)S(1)} %bitcast.65, f32[128,4,128]{2,1,0:T(4,128)S(1)} %bitcast.70, bf16[128,128,4,32]{1,3,2,0:T(8,128)(2,1)} %collective-permute-done.1, f32[128,4,128,128]{2,3,1,0:T(8,128)} %get-tuple-element.321, f32[128,4,128]{2,1,0:T(4,128)S(1)} %max.11, ...), kind=kOutput, calls=%fused_computation.7.clone.1 | convolution fusion | flops 566231040 | bytes 55312384 | tf_op jit(solution)/shard_map/while/body/eval_jaxpr/ihjk,ikhd->ihjd/dot_general | solution.py:47
  228.7 46.0 %collective-permute-done = bf16[128,128,4,32]{1,3,2,0:T(8,128)(2,1)} collective-permute-done((bf16[128,128,4,32]{1,3,2,0:T(8,128)(2,1)}, bf16[128,128,4,32]{1,3,2,0:T(8,128)(2,1)}, u32[]{:S(2)}, u32[]{:S(2)}) %collective-permute-start) | collective-permute-done | bytes 4194336 | tf_op jit(solution)/shard_map/while/body/eval_jaxpr/ppermute | solution.py:56
  274.8 15.9 %add_reduce_fusion.3 = (f32[128,4,128]{2,1,0:T(4,128)S(1)}, f32[128,4,128,128]{2,3,1,0:T(8,128)}) fusion(f32[4,128,128]{1,2,0:T(8,128)S(1)} %constant_dynamic-slice_fusion.2, bf16[128,128,4,32]{1,3,2,0:T(8,128)(2,1)} %get-tuple-element.360, bf16[128,128,4,32]{1,3,2,0:T(8,128)(2,1)} %collective-permute-done), kind=kOutput, calls=%fused_computation.1.clone.1 | convolution fusion | flops 553582592 | bytes 42467328 | tf_op jit(solution)/shard_map/while/body/eval_jaxpr/ijhd,ikhd->ihjk/dot_general | solution.py:42
  290.8 14.8 %fusion.56 = f32[128,4,128]{2,1,0:T(4,128)S(1)} fusion(f32[128,4,128,128]{2,3,1,0:T(8,128)} %get-tuple-element.321, f32[128,4,128]{2,1,0:T(4,128)S(1)} %max.11, f32[4,128,128]{1,2,0:T(8,128)S(1)} %constant_dynamic-slice_fusion.2), kind=kLoop, calls=%fused_computation.3.clone.1 | loop fusion | flops 25100288 | bytes 34340864 | tf_op jit(solution)/shard_map/while/body/eval_jaxpr/reduce_sum | solution.py:46
  305.8 5.9 %copy.46 = bf16[128,128,4,32]{1,3,2,0:T(8,128)(2,1)} copy(bf16[128,128,4,32]{1,3,2,0:T(8,128)(2,1)} %collective-permute-done) | data formatting | bytes 8388608 | tf_op jit(solution)/shard_map/while
  311.8 7.9 %collective-permute-done.1 = bf16[128,128,4,32]{1,3,2,0:T(8,128)(2,1)} collective-permute-done((bf16[128,128,4,32]{1,3,2,0:T(8,128)(2,1)}, bf16[128,128,4,32]{1,3,2,0:T(8,128)(2,1)}, u32[]{:S(2)}, u32[]{:S(2)}) %collective-permute-start.1) | collective-permute-done | bytes 4194336 | tf_op jit(solution)/shard_map/while/body/eval_jaxpr/ppermute | solution.py:56
  325.4 14.8 %multiply_add_fusion.5 = f32[128,4,128,32]{2,3,1,0:T(8,128)S(1)} fusion(f32[128,4,128,32]{2,3,1,0:T(8,128)S(1)} %bitcast.65, f32[128,4,128]{2,1,0:T(4,128)S(1)} %bitcast.70, bf16[128,128,4,32]{1,3,2,0:T(8,128)(2,1)} %collective-permute-done.1, f32[128,4,128,128]{2,3,1,0:T(8,128)} %get-tuple-element.321, f32[128,4,128]{2,1,0:T(4,128)S(1)} %max.11, ...), kind=kOutput, calls=%fused_computation.7.clone.1 | convolution fusion | flops 566231040 | bytes 55312384 | tf_op jit(solution)/shard_map/while/body/eval_jaxpr/ihjk,ikhd->ihjd/dot_general | solution.py:47
  345.3 46.0 %collective-permute-done = bf16[128,128,4,32]{1,3,2,0:T(8,128)(2,1)} collective-permute-done((bf16[128,128,4,32]{1,3,2,0:T(8,128)(2,1)}, bf16[128,128,4,32]{1,3,2,0:T(8,128)(2,1)}, u32[]{:S(2)}, u32[]{:S(2)}) %collective-permute-start) | collective-permute-done | bytes 4194336 | tf_op jit(solution)/shard_map/while/body/eval_jaxpr/ppermute | solution.py:56
  391.3 15.9 %add_reduce_fusion.3 = (f32[128,4,128]{2,1,0:T(4,128)S(1)}, f32[128,4,128,128]{2,3,1,0:T(8,128)}) fusion(f32[4,128,128]{1,2,0:T(8,128)S(1)} %constant_dynamic-slice_fusion.2, bf16[128,128,4,32]{1,3,2,0:T(8,128)(2,1)} %get-tuple-element.360, bf16[128,128,4,32]{1,3,2,0:T(8,128)(2,1)} %collective-permute-done), kind=kOutput, calls=%fused_computation.1.clone.1 | convolution fusion | flops 553582592 | bytes 42467328 | tf_op jit(solution)/shard_map/while/body/eval_jaxpr/ijhd,ikhd->ihjk/dot_general | solution.py:42
  407.3 14.8 %fusion.56 = f32[128,4,128]{2,1,0:T(4,128)S(1)} fusion(f32[128,4,128,128]{2,3,1,0:T(8,128)} %get-tuple-element.321, f32[128,4,128]{2,1,0:T(4,128)S(1)} %max.11, f32[4,128,128]{1,2,0:T(8,128)S(1)} %constant_dynamic-slice_fusion.2), kind=kLoop, calls=%fused_computation.3.clone.1 | loop fusion | flops 25100288 | bytes 34340864 | tf_op jit(solution)/shard_map/while/body/eval_jaxpr/reduce_sum | solution.py:46
  422.4 5.9 %copy.46 = bf16[128,128,4,32]{1,3,2,0:T(8,128)(2,1)} copy(bf16[128,128,4,32]{1,3,2,0:T(8,128)(2,1)} %collective-permute-done) | data formatting | bytes 8388608 | tf_op jit(solution)/shard_map/while
  428.3 7.9 %collective-permute-done.1 = bf16[128,128,4,32]{1,3,2,0:T(8,128)(2,1)} collective-permute-done((bf16[128,128,4,32]{1,3,2,0:T(8,128)(2,1)}, bf16[128,128,4,32]{1,3,2,0:T(8,128)(2,1)}, u32[]{:S(2)}, u32[]{:S(2)}) %collective-permute-start.1) | collective-permute-done | bytes 4194336 | tf_op jit(solution)/shard_map/while/body/eval_jaxpr/ppermute | solution.py:56
  441.9 14.8 %multiply_add_fusion.5 = f32[128,4,128,32]{2,3,1,0:T(8,128)S(1)} fusion(f32[128,4,128,32]{2,3,1,0:T(8,128)S(1)} %bitcast.65, f32[128,4,128]{2,1,0:T(4,128)S(1)} %bitcast.70, bf16[128,128,4,32]{1,3,2,0:T(8,128)(2,1)} %collective-permute-done.1, f32[128,4,128,128]{2,3,1,0:T(8,128)} %get-tuple-element.321, f32[128,4,128]{2,1,0:T(4,128)S(1)} %max.11, ...), kind=kOutput, calls=%fused_computation.7.clone.1 | convolution fusion | flops 566231040 | bytes 55312384 | tf_op jit(solution)/shard_map/while/body/eval_jaxpr/ihjk,ikhd->ihjd/dot_general | solution.py:47
  459.9 8.7 %broadcast_divide_fusion = f32[128,4,128,32]{2,3,1,0:T(8,128)} fusion(f32[128,4,128,32]{2,3,1,0:T(8,128)} %get-tuple-element.229, f32[128,4,128]{2,1,0:T(4,128)S(1)} %get-tuple-element.230), kind=kLoop, calls=%fused_computation.30 | loop fusion | flops 2097152 | bytes 17039360 | tf_op jit(solution)/shard_map/div | solution.py:63
  468.6 9.1 %copy.24 = f32[128,128,128]{2,1,0:T(8,128)} copy(f32[128,128,128]{1,2,0:T(8,128)} %bitcast.71) | data formatting | bytes 16777216 | tf_op jit(solution)/shard_map/reshape | solution.py:63
  477.8 10.5 %fusion.20 = bf16[128,128,128]{2,1,0:T(8,128)(2,1)} fusion(bf16[128,128,128]{2,1,0:T(8,128)(2,1)} %param.12, f32[128,128,128]{2,1,0:T(8,128)} %copy.24, bf16[128,128]{1,0:T(8,128)(2,1)S(1)} %copy-done.12, bf16[128,128]{1,0:T(8,128)(2,1)S(1)} %copy-done.13, f32[128]{0:T(128)S(1)} %copy-done.16, f32[128]{0:T(128)S(1)} %copy-done.18, ...), kind=kOutput, calls=%fused_computation.27 | convolution fusion | flops 1103101952 | bytes 16974848 | tf_op jit(solution)/shard_map/dot_general | solution.py:65
  (88 shorter events, 35.6 us)
Async XLA Ops:
  0.0 36.7 %copy-start = (bf16[128,128]{1,0:T(8,128)(2,1)S(1)}, bf16[128,128]{1,0:T(8,128)(2,1)}, u32[]{:S(2)}) copy-start(bf16[128,128]{1,0:T(8,128)(2,1)} %param.16) | copy-start | bytes 98308
  0.0 9.6 %copy-start.3 = (bf16[128,128,128]{2,1,0:T(8,128)(2,1)S(1)}, bf16[128,128,128]{2,1,0:T(8,128)(2,1)}, u32[]{:S(2)}) copy-start(bf16[128,128,128]{2,1,0:T(8,128)(2,1)} %param.12) | copy-start | bytes 12582916
  0.0 9.6 %copy-start.17 = (f32[128]{0:T(128)S(1)}, f32[128]{0:T(128)}, u32[]{:S(2)}) copy-start(f32[128]{0:T(128)} %param.14) | copy-start | bytes 1540
  0.0 9.6 %copy-start.15 = (f32[128]{0:T(128)S(1)}, f32[128]{0:T(128)}, u32[]{:S(2)}) copy-start(f32[128]{0:T(128)} %param.15) | copy-start | bytes 1540
  0.0 9.6 %copy-start.14 = (bf16[128,4]{0,1:T(4,128)(2,1)S(1)}, bf16[128,4]{0,1:T(4,128)(2,1)}, u32[]{:S(2)}) copy-start(bf16[128,4]{0,1:T(4,128)(2,1)} %param.19) | copy-start | bytes 3076
  3.6 48.8 %copy-start.5 = (f32[128,128]{1,0:T(8,128)}, f32[128,128]{1,0:T(8,128)S(1)}, u32[]{:S(2)}) copy-start(f32[128,128]{1,0:T(8,128)S(1)} %broadcast_multiply_fusion) | copy-start | bytes 196612
  3.6 33.1 %copy-start.9 = (s32[512]{0:T(512)S(1)}, s32[512]{0:T(512)}, u32[]{:S(2)}) copy-start(s32[512]{0:T(512)} %param.13) | copy-start | bytes 6148
  9.7 42.7 %copy-start.7 = (f32[128,128]{1,0:T(8,128)}, f32[128,128]{1,0:T(8,128)S(1)}, u32[]{:S(2)}) copy-start(f32[128,128]{1,0:T(8,128)S(1)} %add_rsqrt_fusion) | copy-start | bytes 196612
  15.5 29.4 %copy-start.10 = (bf16[128,128]{1,0:T(8,128)(2,1)S(1)}, bf16[128,128]{1,0:T(8,128)(2,1)}, u32[]{:S(2)}) copy-start(bf16[128,128]{1,0:T(8,128)(2,1)} %param.17) | copy-start | bytes 98308
  33.0 27.4 %all-to-all-start = ((bf16[512,128,4]{1,2,0:T(4,128)(2,1)}), bf16[512,128,4]{1,2,0:T(4,128)(2,1)S(1)}, u32[]{:S(2)}, u32[]{:S(2)}) async-start(bf16[512,128,4]{1,2,0:T(4,128)(2,1)} %all_gather.3), calls=%async_computation | async-start | bytes 1048576 | tf_op jit(solution)/shard_map/all_to_all | solution.py:35
  36.7 8.2 %copy-start.4 = (bf16[128,128,128]{2,1,0:T(8,128)(2,1)S(1)}, bf16[128,128,128]{2,1,0:T(8,128)(2,1)}, u32[]{:S(2)}) copy-start(bf16[128,128,128]{2,1,0:T(8,128)(2,1)} %param.12) | copy-start | bytes 12582916
  44.9 7.5 %copy-start.11 = (bf16[128,128]{1,0:T(8,128)(2,1)S(1)}, bf16[128,128]{1,0:T(8,128)(2,1)}, u32[]{:S(2)}) copy-start(bf16[128,128]{1,0:T(8,128)(2,1)} %param.18) | copy-start | bytes 98308
  110.3 47.9 %collective-permute-start = (bf16[128,128,4,32]{1,3,2,0:T(8,128)(2,1)}, bf16[128,128,4,32]{1,3,2,0:T(8,128)(2,1)}, u32[]{:S(2)}, u32[]{:S(2)}) collective-permute-start(bf16[128,128,4,32]{1,3,2,0:T(8,128)(2,1)} %get-tuple-element.340), channel_id=1, source_target_pairs={{0,1},{1,2},{2,3},{3,0},{4,5},{5,6},{6,7},{7,4},{8,9},{9,10},{10,1... | collective-permute-start | bytes 12582920 | tf_op jit(solution)/shard_map/while/body/eval_jaxpr/ppermute | solution.py:56
  110.6 92.6 %collective-permute-start.1 = (bf16[128,128,4,32]{1,3,2,0:T(8,128)(2,1)}, bf16[128,128,4,32]{1,3,2,0:T(8,128)(2,1)}, u32[]{:S(2)}, u32[]{:S(2)}) collective-permute-start(bf16[128,128,4,32]{1,3,2,0:T(8,128)(2,1)} %get-tuple-element.341), channel_id=1, source_target_pairs={{0,1},{1,2},{2,3},{3,0},{4,5},{5,6},{6,7},{7,4},{8,9},{9,10},{10,1... | collective-permute-start | bytes 12582920 | tf_op jit(solution)/shard_map/while/body/eval_jaxpr/ppermute | solution.py:56
  189.3 19.6 %slice-start = ((s8[8388608]{0:T(1024)(128)(4,1)}), s8[4194304]{0:T(1024)(128)(4,1)S(1)}, s32[]{:S(2)}) async-start(s8[8388608]{0:T(1024)(128)(4,1)} %bitcast.64), calls=%async_computation.1 | async-start | bytes 8388608 | tf_op jit(solution)/shard_map/while
  195.2 13.6 %slice-start.1 = ((s8[8388608]{0:T(1024)(128)(4,1)}), s8[4194304]{0:T(1024)(128)(4,1)S(1)}, s32[]{:S(2)}) async-start(s8[8388608]{0:T(1024)(128)(4,1)} %bitcast.64), calls=%async_computation.2 | async-start | bytes 8388608 | tf_op jit(solution)/shard_map/while
  226.8 47.9 %collective-permute-start = (bf16[128,128,4,32]{1,3,2,0:T(8,128)(2,1)}, bf16[128,128,4,32]{1,3,2,0:T(8,128)(2,1)}, u32[]{:S(2)}, u32[]{:S(2)}) collective-permute-start(bf16[128,128,4,32]{1,3,2,0:T(8,128)(2,1)} %get-tuple-element.340), channel_id=1, source_target_pairs={{0,1},{1,2},{2,3},{3,0},{4,5},{5,6},{6,7},{7,4},{8,9},{9,10},{10,1... | collective-permute-start | bytes 12582920 | tf_op jit(solution)/shard_map/while/body/eval_jaxpr/ppermute | solution.py:56
  226.8 92.9 %collective-permute-start.1 = (bf16[128,128,4,32]{1,3,2,0:T(8,128)(2,1)}, bf16[128,128,4,32]{1,3,2,0:T(8,128)(2,1)}, u32[]{:S(2)}, u32[]{:S(2)}) collective-permute-start(bf16[128,128,4,32]{1,3,2,0:T(8,128)(2,1)} %get-tuple-element.341), channel_id=1, source_target_pairs={{0,1},{1,2},{2,3},{3,0},{4,5},{5,6},{6,7},{7,4},{8,9},{9,10},{10,1... | collective-permute-start | bytes 12582920 | tf_op jit(solution)/shard_map/while/body/eval_jaxpr/ppermute | solution.py:56
  305.8 19.6 %slice-start = ((s8[8388608]{0:T(1024)(128)(4,1)}), s8[4194304]{0:T(1024)(128)(4,1)S(1)}, s32[]{:S(2)}) async-start(s8[8388608]{0:T(1024)(128)(4,1)} %bitcast.64), calls=%async_computation.1 | async-start | bytes 8388608 | tf_op jit(solution)/shard_map/while
  311.8 13.6 %slice-start.1 = ((s8[8388608]{0:T(1024)(128)(4,1)}), s8[4194304]{0:T(1024)(128)(4,1)S(1)}, s32[]{:S(2)}) async-start(s8[8388608]{0:T(1024)(128)(4,1)} %bitcast.64), calls=%async_computation.2 | async-start | bytes 8388608 | tf_op jit(solution)/shard_map/while
  343.4 47.9 %collective-permute-start = (bf16[128,128,4,32]{1,3,2,0:T(8,128)(2,1)}, bf16[128,128,4,32]{1,3,2,0:T(8,128)(2,1)}, u32[]{:S(2)}, u32[]{:S(2)}) collective-permute-start(bf16[128,128,4,32]{1,3,2,0:T(8,128)(2,1)} %get-tuple-element.340), channel_id=1, source_target_pairs={{0,1},{1,2},{2,3},{3,0},{4,5},{5,6},{6,7},{7,4},{8,9},{9,10},{10,1... | collective-permute-start | bytes 12582920 | tf_op jit(solution)/shard_map/while/body/eval_jaxpr/ppermute | solution.py:56
  343.4 92.9 %collective-permute-start.1 = (bf16[128,128,4,32]{1,3,2,0:T(8,128)(2,1)}, bf16[128,128,4,32]{1,3,2,0:T(8,128)(2,1)}, u32[]{:S(2)}, u32[]{:S(2)}) collective-permute-start(bf16[128,128,4,32]{1,3,2,0:T(8,128)(2,1)} %get-tuple-element.341), channel_id=1, source_target_pairs={{0,1},{1,2},{2,3},{3,0},{4,5},{5,6},{6,7},{7,4},{8,9},{9,10},{10,1... | collective-permute-start | bytes 12582920 | tf_op jit(solution)/shard_map/while/body/eval_jaxpr/ppermute | solution.py:56
  422.4 19.6 %slice-start = ((s8[8388608]{0:T(1024)(128)(4,1)}), s8[4194304]{0:T(1024)(128)(4,1)S(1)}, s32[]{:S(2)}) async-start(s8[8388608]{0:T(1024)(128)(4,1)} %bitcast.64), calls=%async_computation.1 | async-start | bytes 8388608 | tf_op jit(solution)/shard_map/while
  428.3 13.6 %slice-start.1 = ((s8[8388608]{0:T(1024)(128)(4,1)}), s8[4194304]{0:T(1024)(128)(4,1)S(1)}, s32[]{:S(2)}) async-start(s8[8388608]{0:T(1024)(128)(4,1)} %bitcast.64), calls=%async_computation.2 | async-start | bytes 8388608 | tf_op jit(solution)/shard_map/while
  456.7 3.2 copy-start.2
  468.6 9.1 %copy-start.6 = (f32[128,128]{1,0:T(8,128)S(1)}, f32[128,128]{1,0:T(8,128)}, u32[]{:S(2)}) copy-start(f32[128,128]{1,0:T(8,128)} %copy-done.5) | copy-start | bytes 196612
  468.6 9.1 %copy-start.8 = (f32[128,128]{1,0:T(8,128)S(1)}, f32[128,128]{1,0:T(8,128)}, u32[]{:S(2)}) copy-start(f32[128,128]{1,0:T(8,128)} %copy-done.7) | copy-start | bytes 196612
  468.6 9.1 %copy-start.12 = (bf16[128,128]{1,0:T(8,128)(2,1)S(1)}, bf16[128,128]{1,0:T(8,128)(2,1)}, u32[]{:S(2)}) copy-start(bf16[128,128]{1,0:T(8,128)(2,1)} %param.21) | copy-start | bytes 98308
  468.6 9.1 %copy-start.13 = (bf16[128,128]{1,0:T(8,128)(2,1)S(1)}, bf16[128,128]{1,0:T(8,128)(2,1)}, u32[]{:S(2)}) copy-start(bf16[128,128]{1,0:T(8,128)(2,1)} %param.20) | copy-start | bytes 98308
  468.6 9.2 %copy-start.16 = (f32[128]{0:T(128)S(1)}, f32[128]{0:T(128)}, u32[]{:S(2)}) copy-start(f32[128]{0:T(128)} %param.15) | copy-start | bytes 1540
  468.6 9.2 %copy-start.18 = (f32[128]{0:T(128)S(1)}, f32[128]{0:T(128)}, u32[]{:S(2)}) copy-start(f32[128]{0:T(128)} %param.14) | copy-start | bytes 1540
  477.8 10.5 %copy-start.1 = (bf16[128,128]{1,0:T(8,128)(2,1)S(1)}, bf16[128,128]{1,0:T(8,128)(2,1)}, u32[]{:S(2)}) copy-start(bf16[128,128]{1,0:T(8,128)(2,1)} %param.16) | copy-start | bytes 98308
  (2 other events, 6.4 us)
where the time goes:
time: 490 us; the launch traced here: 488 us
  matrix products  166 us (34%)
  waiting for transfers between devices  162 us (33%)
  other arithmetic  78.7 us (16%)
  local copies, waits for them, and re-layouts  54.2 us (11%)
  blocking collectives  17.5 us (4%)
  starting transfers between devices  9.34 us (2%)
    ppermute x6, waiting for transfers between devices, hop_step(): kv_blocks = lax.ppermute(kv_blocks, 'col', shift_pairs)  162 us
    dot_general x4, matrix products, fold_block(): jnp.einsum('ijhd,ikhd->ihjk', queries, key_part, preferred_element_type=j...  63.7 us
    dot_general x4, matrix products, fold_block(): jnp.einsum('ihjk,ikhd->ihjd', weights.astype(jnp.bfloat16), val_part, pre...  62.6 us
    reduce_sum x4, other arithmetic, fold_block(): run_sum = run_sum * rescale + jnp.sum(weights, axis=-1)  59.3 us
    while x27, local copies, waits for them, and re-layouts  44.6 us
    all_gather x1, blocking collectives, per_device(): bias_cols = lax.all_gather(bias_tile, 'row', axis=0, tiled=True)  17.5 us
    dot_general x1, matrix products, per_device(): update = jnp.dot(gated_out, w_o, preferred_element_type=jnp.float32)  10.5 us
  transfers between devices with their start and end apart: 7, of which 6 were waited for; matrix products, arithmetic and copies ran while one was open for 28% of the time, Pallas kernels for 0%

commit v1 on v0

v1 whole, which is shorter than its diff:
```python
import functools

import jax
import jax.numpy as jnp
from jax import lax
from jax.experimental import pallas as pl
from jax.experimental.pallas import tpu as pltpu
from jax.sharding import PartitionSpec as P

LN_EPS = 1e-5
F32 = jnp.float32
BF16 = jnp.bfloat16


def layer_norm(pair_rep, ln_gamma, ln_beta):
    pair_f32 = pair_rep.astype(F32)
    mean_c = jnp.mean(pair_f32, axis=-1, keepdims=True)
    centered = pair_f32 - mean_c
    var_c = jnp.mean(jnp.square(centered), axis=-1, keepdims=True)
    return (centered * lax.rsqrt(var_c + LN_EPS) * ln_gamma + ln_beta).astype(BF16)


def row_kernel(heads, n_q, z_ref, bias_ref, gamma_ref, beta_ref, wkt_ref, wv_ref, wqg_ref, wo_ref, out_ref):
    chan = z_ref.shape[-1]
    proj = wv_ref.shape[1]
    head_dim = proj // heads
    z = z_ref[0]
    a = layer_norm(z, gamma_ref[...], beta_ref[...])
    kt = lax.dot_general(wkt_ref[...], a, (((1,), (1,)), ((), ())), preferred_element_type=F32).astype(BF16)
    v = jnp.dot(a, wv_ref[...], preferred_element_type=F32).astype(BF16)
    qg = jnp.dot(a[:n_q], wqg_ref[...], preferred_element_type=F32)
    q = (qg[:, :proj] * head_dim ** -0.5).astype(BF16)
    gate = jax.nn.sigmoid(qg[:, proj:])
    lane_head = lax.broadcasted_iota(jnp.int32, (1, proj), 1) // head_dim
    att = jnp.zeros((n_q, proj), F32)
    for h in range(heads):
        mine = lane_head == h
        qh = jnp.where(mine, q, jnp.zeros_like(q))
        s = jnp.dot(qh, kt, preferred_element_type=F32) + bias_ref[h]
        m = jnp.max(s, axis=-1, keepdims=True)
        p = jnp.exp(s - m)
        l = jnp.sum(p, axis=-1, keepdims=True)
        o = jnp.dot(p.astype(BF16), v, preferred_element_type=F32)
        att = jnp.where(mine, o / l, att)
    go = (gate * att).astype(BF16)
    upd = jnp.dot(go, wo_ref[...], preferred_element_type=F32)
    out_ref[0] = (z[:n_q].astype(F32) + upd).astype(BF16)


def solution(mesh):
    col_size = mesh.shape['col']
    tile_spec = P(('dp', 'row'), 'col', None)
    partner_pairs = [(d, d ^ 1) for d in range(col_size)]

    def per_device(pair_tile, res_mask, ln_gamma, ln_beta, w_q, w_k, w_v, w_b, w_g, w_o):
        row_len, col_len, chan = pair_tile.shape
        heads = w_b.shape[1]
        proj = w_q.shape[1]
        col_idx = lax.axis_index('col')
        core = col_idx % 2
        half = row_len // 2
        n_q = 2 * col_len
        n_k = col_size * col_len
        shift = (col_idx // 2) * n_q

        normed = layer_norm(pair_tile, ln_gamma, ln_beta)
        bias_tile = jnp.dot(normed, w_b, preferred_element_type=F32).astype(BF16)
        bias_cols = lax.all_gather(bias_tile, 'row', axis=0, tiled=True)
        bias_rows = lax.all_to_all(bias_cols, 'col', 0, 1, tiled=True)
        bias_rows = jnp.transpose(bias_rows, (2, 0, 1))
        other = lax.ppermute(bias_rows, 'col', partner_pairs)
        both = jnp.where(core == 0, jnp.concatenate([bias_rows, other], 1), jnp.concatenate([other, bias_rows], 1))
        key_bias = jnp.where(res_mask > 0, 0.0, -1e9).astype(F32)
        full_bias = both.astype(F32) + key_bias
        full_bias = jnp.where(shift > 0, jnp.roll(full_bias, -n_q, 2), full_bias)

        z_all = lax.all_gather(pair_tile, 'col', axis=1, tiled=True)
        z_half = lax.dynamic_slice_in_dim(z_all, core * half, half, 0)
        z_half = jnp.where(shift > 0, jnp.roll(z_half, -n_q, 1), z_half)

        full = lambda *shape: pl.BlockSpec(shape, lambda i: (0,) * len(shape))
        out = pl.pallas_call(
            functools.partial(row_kernel, heads, n_q),
            grid=(half,),
            in_specs=[
                pl.BlockSpec((1, n_k, chan), lambda i: (i, 0, 0)),
                full(heads, n_q, n_k), full(1, chan), full(1, chan),
                full(proj, chan), full(chan, proj), full(chan, 2 * proj), full(proj, chan),
            ],
            out_specs=pl.BlockSpec((1, n_q, chan), lambda i: (i, 0, 0)),
            out_shape=jax.ShapeDtypeStruct((half, n_q, chan), BF16),
            compiler_params=pltpu.CompilerParams(vmem_limit_bytes=60 * 1024 * 1024),
        )(z_half, full_bias, ln_gamma.reshape(1, -1), ln_beta.reshape(1, -1), w_k.T, w_v, jnp.concatenate([w_q, w_g], 1), w_o)
        mine = lax.dynamic_slice_in_dim(out, core * col_len, col_len, 1)
        theirs = lax.dynamic_slice_in_dim(out, (1 - core) * col_len, col_len, 1)
        got = lax.ppermute(theirs, 'col', partner_pairs)
        return jnp.where(core == 0, jnp.concatenate([mine, got], 0), jnp.concatenate([got, mine], 0))

    return jax.shard_map(per_device, mesh=mesh, in_specs=(tile_spec, P('dp'), P(), P(), P(), P(), P(), P(), P(), P()), out_specs=tile_spec, check_vma=False)
```

time: 490 us -> 276 us (0.56)
  matrix products: 166 us -> 5.84 us
  Pallas kernels: 0 us -> 123 us
  waiting for transfers between devices: 162 us -> 68.2 us
  other arithmetic: 78.7 us -> 21.8 us
  local copies, waits for them, and re-layouts: 54.2 us -> 8.36 us
  blocking collectives: 17.5 us -> 34.8 us
  between operations: 0.25 us -> 13.6 us
  starting transfers between devices: 9.34 us -> 0.39 us
    dot_general x13 -> x1, matrix products: 166 us -> 5.84 us  [per_device(): bias_tile = jnp.dot(normed, w_b, preferred_element_type=F32).astype(BF16)]
    ppermute x6 -> x2, waiting for transfers between devices: 162 us -> 4.41 us  [the longest x1 3.91 us: per_device(): got = lax.ppermute(theirs, 'col', partner_pairs)]
    pallas_call x0 -> x1, Pallas kernels: none -> 123 us  [per_device(): pl.pallas_call(functools.partial(row_kernel, heads, n_q), grid=(half,), i...]
    all_gather x0 -> x1, waiting for transfers between devices: none -> 63.1 us  [per_device(): z_all = lax.all_gather(pair_tile, 'col', axis=1, tiled=True)]
    reduce_sum x4 -> x0, other arithmetic: 59.3 us -> none  [fold_block(): run_sum = run_sum * rescale + jnp.sum(weights, axis=-1)]
    while x27 -> x0, local copies, waits for them, and re-layouts: 44.6 us -> none
    all_to_all x0 -> x1, blocking collectives: none -> 17.4 us  [per_device(): bias_rows = lax.all_to_all(bias_cols, 'col', 0, 1, tiled=True)]
    select_n x1 -> x4, other arithmetic: 0.01 us -> 12.6 us  [the longest x1 8.45 us: per_device(): z_half = jnp.where(shift > 0, jnp.roll(z_half, -n_q, 1), z_half)]
  transfers between devices with their start and end apart: 7 -> 3, of which waited for: 6 -> 3; matrix products, arithmetic and copies ran while one was open for 28% -> 7% of each run, Pallas kernels for 0% -> 0%
where the time goes in v1:
time: 276 us
  Pallas kernels  123 us (45%)
  waiting for transfers between devices  68.2 us (25%)
  blocking collectives  34.8 us (13%)
  other arithmetic  21.8 us (8%)
  between operations  13.6 us (5%)
  local copies, waits for them, and re-layouts  8.36 us (3%)
  matrix products  5.84 us (2%)
    pallas_call x1, Pallas kernels, per_device(): pl.pallas_call(functools.partial(row_kernel, heads, n_q), grid=(half,), i...  123 us
    all_gather x1, waiting for transfers between devices, per_device(): z_all = lax.all_gather(pair_tile, 'col', axis=1, tiled=True)  63.1 us
    all_gather x1, blocking collectives, per_device(): bias_cols = lax.all_gather(bias_tile, 'row', axis=0, tiled=True)  17.4 us
    all_to_all x1, blocking collectives, per_device(): bias_rows = lax.all_to_all(bias_cols, 'col', 0, 1, tiled=True)  17.4 us
    select_n x1, other arithmetic, per_device(): z_half = jnp.where(shift > 0, jnp.roll(z_half, -n_q, 1), z_half)  8.45 us
    dot_general x1, matrix products, per_device(): bias_tile = jnp.dot(normed, w_b, preferred_element_type=F32).astype(BF16)  5.84 us
  transfers between devices with their start and end apart: 3, of which 3 were waited for; matrix products, arithmetic and copies ran while one was open for 7% of the time, Pallas kernels for 0%

profile of v1, /device:TPU:0, one launch (start us, length us, event | category | flops | bytes accessed | tf_op | source)
XLA Modules:
  0.0 276.1 jit_solution(4651931494836950793)
XLA Ops:
  6.5 0.0 copy-start
  6.5 0.0 all-gather.2.cloned.1.call-start
  6.5 0.7 all-gather.2.cloned.1.call-update
  7.3 0.0 copy-start.6
  7.3 0.0 copy-start.7
  7.3 3.5 %convert_reduce_fusion = f32[128,128]{1,0:T(8,128)S(1)} fusion(bf16[128,128,128]{2,1,0:T(8,128)(2,1)} %param.10), kind=kLoop, calls=%fused_computation.1 | loop fusion | flops 4177920 | bytes 4259840 | tf_op jit(solution)/shard_map/reduce_sum | solution.py:17
  10.8 4.8 %fusion.2 = f32[128,128]{1,0:T(8,128)S(1)} fusion(bf16[128,128,128]{2,1,0:T(8,128)(2,1)S(1)} %copy-done.1, f32[128,128]{1,0:T(8,128)S(1)} %broadcast_multiply_fusion), kind=kLoop, calls=%fused_computation.4 | loop fusion | flops 8372224 | bytes 4325376 | tf_op jit(solution)/shard_map/reduce_sum | solution.py:19
  15.7 0.0 copy-start.2
  15.7 0.0 copy-start.3
  15.7 0.0 copy-start.4
  15.7 0.0 copy-start.5
  15.7 5.8 %fusion.8 = bf16[128,128,4]{1,2,0:T(4,128)(2,1)S(1)} fusion(bf16[128,128,128]{2,1,0:T(8,128)(2,1)S(1)} %copy-done.1, f32[128]{0:T(128)S(1)} %copy-done.6, f32[128]{0:T(128)S(1)} %copy-done.7, f32[128,128]{1,0:T(8,128)S(1)} %add_rsqrt_fusion, f32[128,128]{1,0:T(8,128)S(1)} %broadcast_multiply_fusion, bf16[128,4]{0,1:T(4,128)(2,1)S(1)} %copy-done), kind=kOutput, calls=%fused_computation.13 | convolution fusion | flops 29425664 | bytes 4458496 | tf_op jit(solution)/shard_map/dot_general | solution.py:67
  21.5 17.4 %all_gather.7 = bf16[512,128,4]{1,2,0:T(4,128)(2,1)S(1)} all-gather(bf16[128,128,4]{1,2,0:T(4,128)(2,1)S(1)} %fusion.8), channel_id=1, replica_groups=mesh['dp'=2,'row'=4,'col'=4] {'row'}, dimensions={0}, use_global_device_ids=true | all-gather | bytes 655360 | tf_op jit(solution)/shard_map/all_gather | solution.py:68
  38.9 17.4 %all_to_all.18 = bf16[512,128,4]{1,2,0:T(4,128)(2,1)S(1)} all-to-all(bf16[512,128,4]{1,2,0:T(4,128)(2,1)S(1)} %all_gather.7), channel_id=1, replica_groups=mesh['dp'=2,'row'=4,'col'=4] {'col'}, dimensions={0} | all-to-all | bytes 1048576 | tf_op jit(solution)/shard_map/all_to_all | solution.py:69
  56.3 0.4 copy.16
  56.8 0.2 all_to_all.16
  57.0 0.1 collective-permute-start
  57.1 0.7 copy.14
  57.8 0.0 copy-done.3
  57.8 0.6 pad_maximum_fusion.wqg_ref
  58.4 0.5 collective-permute-done
  58.9 0.4 convert_add_fusion
  59.3 0.2 fusion.12
  59.5 1.8 maximum_select_fusion.2.bias_ref
  61.3 63.1 %all-gather.2.cloned.1.call-done = bf16[128,512,128]{2,1,0:T(8,128)(2,1)} async-done(((bf16[128,128,128]{2,1,0:T(8,128)(2,1)}), bf16[128,512,128]{2,1,0:T(8,128)(2,1)}) %all-gather.2.cloned.1.call-update) | async-done | bytes 16777232 | tf_op jit(solution)/shard_map/all_gather | solution.py:77
  124.3 4.1 %constant_dynamic-slice_fusion.1 = (bf16[64,256,128]{2,1,0:T(8,128)(2,1)S(1)}, bf16[64,256,128]{2,1,0:T(8,128)(2,1)S(1)}) fusion(bf16[128,512,128]{2,1,0:T(8,128)(2,1)} %all-gather.2.cloned.1.call-done, s32[]{:T(128)S(6)} %select_n.60, s32[]{:T(128)S(6)} %add.51), kind=kLoop, calls=%fused_computation.21 | loop fusion | bytes 16777224 | tf_op jit(solution)/shard_map/jit(_roll_static)/slice | solution.py:79
  128.4 8.4 %maximum_select_fusion.z_ref = bf16[64,512,128]{2,1,0:T(8,128)(2,1)} fusion(bf16[64,256,128]{2,1,0:T(8,128)(2,1)S(1)} %get-tuple-element.6, bf16[64,256,128]{2,1,0:T(8,128)(2,1)S(1)} %get-tuple-element.5, bf16[128,512,128]{2,1,0:T(8,128)(2,1)} %all-gather.2.cloned.1.call-done, s32[]{:T(128)S(6)} %select_n.60, pred[]{:T(512)S(6)} %gt.10), kind=kLoop, calls=%fused_computation.8 | loop fusion | flops 20971520 | bytes 25165828 | tf_op jit(solution)/shard_map/jit(_where)/select_n | solution.py:79
  136.9 123.1 %shard_map.100 = bf16[64,256,128]{2,1,0:T(8,128)(2,1)} custom-call(bf16[64,512,128]{2,1,0:T(8,128)(2,1)} %maximum_select_fusion.z_ref, f32[4,256,512]{2,1,0:T(8,128)} %maximum_select_fusion.2.bias_ref, f32[1,128]{1,0:T(1,128)} %bitcast.20, f32[1,128]{1,0:T(1,128)} %bitcast.19, bf16[128,128]{1,0:T(8,128)(2,1)} %bitcast.18, bf16[128,128]{1,0:T(8,128)(2,1)} %wv_ref.1, ...), custom_call_target="tpu_custom_call" | custom-call | tf_op jit(solution)/shard_map/pallas_call | solution.py:82
  260.0 2.7 constant_dynamic-slice_fusion.3
  262.7 0.3 collective-permute-start.1
  263.0 3.9 %collective-permute-done.1 = bf16[64,128,128]{2,1,0:T(8,128)(2,1)S(1)} collective-permute-done((bf16[64,128,128]{2,1,0:T(8,128)(2,1)S(1)}, bf16[64,128,128]{2,1,0:T(8,128)(2,1)S(1)}, u32[]{:S(2)}, u32[]{:S(2)}) %collective-permute-start.1) | collective-permute-done | bytes 2097184 | tf_op jit(solution)/shard_map/ppermute | solution.py:96
  266.9 2.3 maximum_select_fusion.1
  (11 shorter events, 0.0 us)
Async XLA Ops:
  6.5 9.1 %copy-start = (bf16[128,4]{0,1:T(4,128)(2,1)S(1)}, bf16[128,4]{0,1:T(4,128)(2,1)}, u32[]{:S(2)}) copy-start(bf16[128,4]{0,1:T(4,128)(2,1)} %param.17) | copy-start | bytes 3076
  6.5 117.8 %all-gather.2.cloned.1.call-start = ((), (), s32[]{:S(2)}) async-start(), calls=%async_computation.1 | async-start | bytes 20971520 | tf_op jit(solution)/shard_map/all_gather | solution.py:77
  7.3 3.6 %copy-start.1 = (bf16[128,128,128]{2,1,0:T(8,128)(2,1)S(1)}, bf16[128,128,128]{2,1,0:T(8,128)(2,1)}, u32[]{:S(2)}) copy-start(bf16[128,128,128]{2,1,0:T(8,128)(2,1)} %param.10) | copy-start | bytes 12582916
  7.3 8.4 %copy-start.6 = (f32[128]{0:T(128)S(1)}, f32[128]{0:T(128)}, u32[]{:S(2)}) copy-start(f32[128]{0:T(128)} %param.13) | copy-start | bytes 1540
  7.3 8.4 %copy-start.7 = (f32[128]{0:T(128)S(1)}, f32[128]{0:T(128)}, u32[]{:S(2)}) copy-start(f32[128]{0:T(128)} %param.12) | copy-start | bytes 1540
  15.7 41.4 %copy-start.2 = (bf16[128,128]{1,0:T(8,128)(2,1)S(1)}, bf16[128,128]{1,0:T(8,128)(2,1)}, u32[]{:S(2)}) copy-start(bf16[128,128]{1,0:T(8,128)(2,1)} %param.15) | copy-start | bytes 98308
  15.7 42.1 %copy-start.3 = (bf16[128,128]{1,0:T(8,128)(2,1)S(1)}, bf16[128,128]{1,0:T(8,128)(2,1)}, u32[]{:S(2)}) copy-start(bf16[128,128]{1,0:T(8,128)(2,1)} %param.18) | copy-start | bytes 98308
  15.7 42.1 %copy-start.4 = (bf16[128,128]{1,0:T(8,128)(2,1)S(1)}, bf16[128,128]{1,0:T(8,128)(2,1)}, u32[]{:S(2)}) copy-start(bf16[128,128]{1,0:T(8,128)(2,1)} %param.14) | copy-start | bytes 98308
  15.7 42.7 %copy-start.5 = (s32[512]{0:T(512)S(1)}, s32[512]{0:T(512)}, u32[]{:S(2)}) copy-start(s32[512]{0:T(512)} %param.11) | copy-start | bytes 6148
  57.0 2.0 collective-permute-start
  262.7 4.2 %collective-permute-start.1 = (bf16[64,128,128]{2,1,0:T(8,128)(2,1)S(1)}, bf16[64,128,128]{2,1,0:T(8,128)(2,1)S(1)}, u32[]{:S(2)}, u32[]{:S(2)}) collective-permute-start(bf16[64,128,128]{2,1,0:T(8,128)(2,1)S(1)} %get-tuple-element.8), channel_id=1, source_target_pairs={{0,1},{1,0},{2,3},{3,2},{4,5},{5,4},{6,7},{7,6},{8,9},{9,8},{10,11... | collective-permute-start | bytes 6291464 | tf_op jit(solution)/shard_map/ppermute | solution.py:96
Sparse Core Ops, SparseCore 0:
  8.9 115.4 all-gather.1

commit v2 on v0

v2 whole, which is shorter than its diff:
```python
import functools

import jax
import jax.numpy as jnp
from jax import lax
from jax.experimental import pallas as pl
from jax.experimental.pallas import tpu as pltpu
from jax.sharding import PartitionSpec as P

LN_EPS = 1e-5
F32 = jnp.float32
BF16 = jnp.bfloat16
NT = (((1,), (1,)), ((), ()))
TN = (((0,), (0,)), ((), ()))
LOG2E = 1.4426950408889634
CORES = 2
SEND_ROWS = 2
OUT_ROWS = 4
EARLY = 4


def layer_norm(z, gamma, beta):
    x = z.astype(F32)
    centered = x - jnp.mean(x, axis=-1, keepdims=True)
    var = jnp.mean(jnp.square(centered), axis=-1, keepdims=True)
    return (centered * lax.rsqrt(var + LN_EPS) * gamma + beta).astype(BF16)


def over_keys(x, op):
    n, width = x.shape
    groups = 8
    t = op(x.reshape(groups, n // 8 // groups, 8, width), axis=1)
    return op(op(t, axis=0), axis=0, keepdims=True)


def kernel(heads, z_hbm, mask_ref, gamma_ref, beta_ref, wk_ref, wt_ref, wb_ref, wo_ref, out_hbm,
           zbuf, own, outv, bias, btile, bsend, brow, a0, a1, k0, k1, v0, v1, q0, q1, g0, g1,
           s0, s1, s2, s3, go,
           local_sem, zp_send, zp_recv, zs_send, zs_recv, b1_send, b1_recv, b2_send, b2_recv,
           b3_send, b3_recv, o_local, o_send, o_recv):
    rows_all, width, chan = z_hbm.shape
    rows = rows_all // CORES
    n_q = CORES * width
    proj = wk_ref.shape[1]
    hd = proj // heads
    steps = rows // SEND_ROWS
    dp, row, col = lax.axis_index('dp'), lax.axis_index('row'), lax.axis_index('col')
    n_row = lax.axis_size('row')
    core, chip = lax.rem(col, CORES), col // CORES
    partner = chip * CORES + 1 - core
    far = (1 - chip) * CORES
    home_chip = row // CORES
    jslot = lax.rem(row, CORES)
    home = chip == home_chip

    def remote(src, dst, send, recv, r, c):
        return pltpu.make_async_remote_copy(src, dst, send, recv, device_id=(dp, r, c),
                                            device_id_type=pl.DeviceIdType.MESH)

    barrier = pltpu.get_barrier_semaphore()
    peers = [(row, partner), (row, far), (row, far + 1)]
    peers += [(lax.rem(row + d, n_row), col) for d in range(1, 4)]
    for r, c in peers:
        pl.semaphore_signal(barrier, inc=1, device_id=(dp, r, c), device_id_type=pl.DeviceIdType.MESH)

    own_copy = pltpu.make_async_copy(z_hbm, own, local_sem.at[0])
    own_copy.start()
    mine_at = pl.ds(pl.multiple_of(core * width, width), width)
    theirs_at = pl.ds(pl.multiple_of((1 - core) * width, width), width)
    far_at = pl.ds(pl.multiple_of((CORES + core) * width, width), width)
    z_copy = pltpu.make_async_copy(z_hbm.at[pl.ds(core * rows, rows)], zbuf.at[:, mine_at, :], local_sem.at[1])
    z_copy.start()
    pl.semaphore_wait(barrier, len(peers))

    to_partner = remote(z_hbm.at[pl.ds((1 - core) * rows, rows)], zbuf.at[:, mine_at, :], zp_send, zp_recv, row, partner)

    def z_send(g, k):
        return remote(z_hbm.at[pl.ds(k * rows + g * SEND_ROWS, SEND_ROWS)],
                      zbuf.at[pl.ds(g * SEND_ROWS, SEND_ROWS), far_at, :],
                      zs_send.at[k, g], zs_recv.at[core, g], row, far + k)

    def z_wait(g):
        for k in range(CORES):
            at = pl.ds((CORES + k) * width, width)
            remote(z_hbm.at[pl.ds(0, SEND_ROWS)], zbuf.at[pl.ds(g * SEND_ROWS, SEND_ROWS), at, :],
                   zs_send.at[k, g], zs_recv.at[k, g], row, far + k).wait_recv()

    def send_step(g, carry):
        for k in range(CORES):
            z_send(g, k).start()
        return carry

    lax.fori_loop(0, EARLY, send_step, 0)
    to_partner.start()

    own_copy.wait()
    batch = 8

    def bias_step(i, carry):
        a = layer_norm(own[pl.ds(i * batch, batch)].reshape(batch * width, chan), gamma_ref[...], beta_ref[...])
        t = lax.dot_general(wb_ref[...], a, NT, preferred_element_type=F32)
        for j in range(batch):
            for h in range(heads):
                brow[h, pl.ds(i * batch + j, 1), :] = t[h:h + 1, j * width:(j + 1) * width]
        return carry

    lax.fori_loop(0, rows_all // batch, bias_step, 0)
    home_slot = core * CORES + jslot
    cross_slot = (CORES + core) * CORES + jslot
    for h in range(heads):
        tile = brow[h].T.astype(BF16)
        bsend[h] = tile

        @pl.when(home)
        def _():
            btile[home_slot, h] = tile

    masks = []
    for s in range(2 * CORES):
        block = chip * CORES + s if s < CORES else far + s - CORES
        m = mask_ref[:, pl.ds(pl.multiple_of(block * width, width), width)]
        masks.append(jnp.broadcast_to(jnp.where(m > 0, 0.0, -1e9).astype(F32), (width, width)).T)

    cross = remote(bsend, btile.at[cross_slot], b1_send, b1_recv, row, far + core)

    @pl.when(jnp.logical_not(home))
    def _():
        cross.start()

    lax.fori_loop(EARLY, steps, send_step, 0)

    def spread(t, d):
        src = bsend if t == 0 else btile.at[cross_slot]
        slot = home_slot if t == 0 else cross_slot
        return remote(src, btile.at[slot], b2_send.at[t, d - 1], b2_recv.at[t, jslot], lax.rem(row + d, n_row), col)

    @pl.when(home)
    def _():
        for d in range(1, 4):
            spread(0, d).start()
        cross.wait_recv()
        for d in range(1, 4):
            spread(1, d).start()

    def forward(t, j):
        slot = (core + CORES * t) * CORES + j
        return remote(btile.at[slot], btile.at[slot], b3_send.at[t, j], b3_recv.at[t, j], row, partner)

    for j in range(CORES):
        for t in range(2):
            slot = (core + CORES * t) * CORES + j

            @pl.when(row != chip * CORES + j)
            def _():
                remote(bsend, btile.at[slot], b1_send, b2_recv.at[t, j], row, partner).wait_recv()

            forward(t, j).start()
    for j in range(CORES):
        for t in range(2):
            slot = (1 - core + CORES * t) * CORES + j
            remote(bsend, btile.at[slot], b1_send, b3_recv.at[t, j], row, partner).wait_recv()

    for s in range(2 * CORES):
        for j in range(CORES):
            for h in range(heads):
                b = btile[s * CORES + j, h].astype(F32)
                bias[h, s * width:(s + 1) * width, j * width:(j + 1) * width] = (b + masks[s]) * LOG2E

    a_s, k_s, v_s, q_s, g_s, sc = (a0, a1), (k0, k1), (v0, v1), (q0, q1), (g0, g1), (s0, s1, s2, s3)
    scale = hd ** -0.5 * LOG2E

    def scores(slot, h):
        part = q_s[slot][h * hd:(h + 1) * hd, :]
        none = jnp.zeros_like(part)
        rhs = jnp.concatenate([part if i == h else none for i in range(heads)], axis=0)
        sc[h][...] = jnp.dot(k_s[slot][...], rhs, preferred_element_type=F32) + bias[h]

    def finish(r):
        upd = lax.dot_general(go[...], wo_ref[...], TN, preferred_element_type=F32)
        outv[r] = (zbuf[r, :n_q].astype(F32) + upd).astype(BF16)

    def out_copies(g):
        src = pl.ds(g * OUT_ROWS, OUT_ROWS)
        dst = out_hbm.at[pl.ds(core * rows + g * OUT_ROWS, OUT_ROWS)]
        return (pltpu.make_async_copy(outv.at[src, mine_at, :], dst, o_local.at[g]),
                remote(outv.at[src, theirs_at, :], dst, o_send.at[g], o_recv.at[g], row, partner))

    def step(i, carry):
        @pl.when(i < steps - 1)
        def _():
            z_wait(i + 1)

        lead = OUT_ROWS // 2 + 1

        @pl.when(jnp.logical_and(i >= lead, lax.rem(i - lead + OUT_ROWS, OUT_ROWS // 2) == 0))
        def _():
            for c in out_copies((i - lead) // (OUT_ROWS // 2)):
                c.start()

        for r in range(2):
            cur, nxt = r, 1 - r
            finish(jnp.maximum(2 * i + r - 1, 0))
            a_s[cur][...] = layer_norm(zbuf[jnp.minimum(2 * i + r + 2, rows - 1)], gamma_ref[...], beta_ref[...])
            a = a_s[nxt]
            for h in range(heads):
                if h < 2:
                    scores(cur, h + 2)
                else:
                    scores(nxt, h - 2)
                if h == 0:
                    k_s[nxt][...] = jnp.dot(a[...], wk_ref[...], preferred_element_type=F32).astype(BF16)
                    t = lax.dot_general(wt_ref[proj:2 * proj], a[:n_q], NT, preferred_element_type=F32)
                    q_s[nxt][...] = (t * scale).astype(BF16)
                if h == 1:
                    t = lax.dot_general(wt_ref[2 * proj:], a[:n_q], NT, preferred_element_type=F32)
                    g_s[nxt][...] = jax.nn.sigmoid(t)
                if h == 2:
                    t = lax.dot_general(wt_ref[:proj], a[...], NT, preferred_element_type=F32)
                    v_s[nxt][...] = t.astype(BF16)
                s = sc[h][...]
                p = jnp.exp2(s - over_keys(s, jnp.max))
                total = over_keys(p, jnp.sum)
                at = slice(h * hd, (h + 1) * hd)
                o = jnp.dot(v_s[cur][at, :], p.astype(BF16), preferred_element_type=F32)
                go[at, :] = (g_s[cur][at, :] * (o / total)).astype(BF16)
        return carry

    pltpu.make_async_copy(z_hbm.at[pl.ds(0, rows)], zbuf.at[:, mine_at, :], local_sem.at[1]).wait()
    to_partner_wait = remote(z_hbm.at[pl.ds(0, rows)], zbuf.at[:, theirs_at, :], zp_send, zp_recv, row, partner)
    to_partner_wait.wait_recv()
    lax.fori_loop(-1, steps, step, 0)
    finish(rows - 1)
    to_partner.wait_send()

    def sent(g, carry):
        for k in range(CORES):
            z_send(g, k).wait_send()
        return carry

    lax.fori_loop(0, steps, sent, 0)
    groups = rows // OUT_ROWS
    for c in out_copies(groups - 1):
        c.start()

    @pl.when(jnp.logical_not(home))
    def _():
        cross.wait_send()

    @pl.when(home)
    def _():
        for t in range(2):
            for d in range(1, 4):
                spread(t, d).wait_send()

    for j in range(CORES):
        for t in range(2):
            forward(t, j).wait_send()

    def drained(g, carry):
        mine, theirs = out_copies(g)
        mine.wait()
        theirs.wait_send()
        remote(outv.at[pl.ds(0, OUT_ROWS), theirs_at, :],
               out_hbm.at[pl.ds((1 - core) * rows + g * OUT_ROWS, OUT_ROWS)],
               o_send.at[g], o_recv.at[g], row, partner).wait_recv()
        return carry

    lax.fori_loop(0, groups, drained, 0)


def solution(mesh):
    tile_spec = P(('dp', 'row'), 'col', None)

    def per_device(pair_tile, res_mask, ln_gamma, ln_beta, w_q, w_k, w_v, w_b, w_g, w_o):
        row_len, width, chan = pair_tile.shape
        heads, proj = w_b.shape[1], w_q.shape[1]
        hd = proj // heads
        rows, n_q = row_len // CORES, CORES * width
        n_k = mesh.shape['col'] * width
        steps, groups = rows // SEND_ROWS, rows // OUT_ROWS
        vmem = pltpu.VMEM
        dma = pltpu.SemaphoreType.DMA
        pairs = lambda *s: [vmem(*s)] * 2
        whole = pl.BlockSpec(memory_space=pltpu.VMEM)
        hbm = pl.BlockSpec(memory_space=pl.ANY)
        return pl.pallas_call(
            functools.partial(kernel, heads),
            in_specs=[hbm] + [whole] * 7,
            out_specs=hbm,
            out_shape=jax.ShapeDtypeStruct(pair_tile.shape, BF16),
            scratch_shapes=[
                vmem((rows, n_k, chan), BF16), vmem((row_len, width, chan), BF16), vmem((rows, n_q, chan), BF16),
                vmem((heads, n_k, n_q), F32), vmem((8, heads, width, width), BF16), vmem((heads, width, width), BF16),
                vmem((heads, width, width), F32),
                *pairs((n_k, chan), BF16), *pairs((n_k, proj), BF16), *pairs((proj, n_k), BF16),
                *pairs((proj, n_q), BF16), *pairs((proj, n_q), F32),
                *[vmem((n_k, n_q), F32)] * 4, vmem((proj, n_q), BF16),
                dma((2,)), dma, dma, dma((CORES, steps)), dma((CORES, steps)), dma, dma, dma((2, 3)), dma((2, CORES)),
                dma((2, CORES)), dma((2, CORES)), dma((groups,)), dma((groups,)), dma((groups,)),
            ],
            compiler_params=pltpu.CompilerParams(collective_id=0, has_side_effects=True, vmem_limit_bytes=56 * 1024 * 1024),
        )(pair_tile, res_mask.reshape(1, -1), ln_gamma.reshape(1, -1), ln_beta.reshape(1, -1), w_k,
          jnp.concatenate([w_v.T, w_q.T, w_g.T], 0), jnp.pad(w_b.T, ((0, 8 - heads), (0, 0))), w_o)

    return jax.shard_map(per_device, mesh=mesh, in_specs=(tile_spec, P('dp'), P(), P(), P(), P(), P(), P(), P(), P()), out_specs=tile_spec, check_vma=False)
```

time: 490 us -> 116 us (0.24)
  matrix products: 166 us -> 0 us
  waiting for transfers between devices: 162 us -> 0 us
  Pallas kernels: 0 us -> 107 us
  other arithmetic: 78.7 us -> 0.66 us
  local copies, waits for them, and re-layouts: 54.2 us -> 8.65 us
  blocking collectives: 17.5 us -> 0 us
  starting transfers between devices: 9.34 us -> 0 us
    dot_general x13 -> x0, matrix products: 166 us -> none  [the longest x4 63.7 us: fold_block(): jnp.einsum('ijhd,ikhd->ihjk', queries, key_part, preferred_element_type=j...]
    ppermute x6 -> x0, waiting for transfers between devices: 162 us -> none  [hop_step(): kv_blocks = lax.ppermute(kv_blocks, 'col', shift_pairs)]
    pallas_call x0 -> x1, Pallas kernels: none -> 107 us  [per_device(): pl.pallas_call(functools.partial(kernel, heads), in_specs=[hbm] + [whole]...]
    reduce_sum x6 -> x0, other arithmetic: 68.8 us -> none  [the longest x4 59.3 us: fold_block(): run_sum = run_sum * rescale + jnp.sum(weights, axis=-1)]
    while x27 -> x0, local copies, waits for them, and re-layouts: 44.6 us -> none
    all_gather x1 -> x0, blocking collectives: 17.5 us -> none  [per_device(): bias_cols = lax.all_gather(bias_tile, 'row', axis=0, tiled=True)]
    reshape x1 -> x0, local copies, waits for them, and re-layouts: 9.11 us -> none  [per_device(): jnp.transpose(acc_out / run_sum[..., None], (0, 2, 1, 3))]
    div x2 -> x0, other arithmetic: 8.66 us -> none  [the longest x1 8.65 us: per_device(): acc_out / run_sum[..., None]]
  transfers between devices with their start and end apart: 7 -> 0, of which waited for: 6 -> 0; matrix products, arithmetic and copies ran while one was open for 28% -> 0% of each run, Pallas kernels for 0% -> 0%
where the time goes in v2:
time: 116 us
  Pallas kernels  107 us (92%)
  local copies, waits for them, and re-layouts  8.65 us (7%)
    pallas_call x1, Pallas kernels, per_device(): pl.pallas_call(functools.partial(kernel, heads), in_specs=[hbm] + [whole]...  107 us
    unnamed x4, local copies, waits for them, and re-layouts  7.39 us

profile of v2, /device:TPU:0, one launch (start us, length us, event | category | flops | bytes accessed | tf_op | source)
XLA Modules:
  0.0 116.0 jit_solution(18139338048759640136)
XLA Ops:
  0.0 1.3 %pad.4.wb_ref = bf16[8,128]{1,0:T(8,128)(2,1)} pad(bf16[4,128]{1,0:T(4,128)(2,1)} %bitcast.11, bf16[]{:T(256)} %constant.2.clone.1), padding=0_4x0_0 | pad | bytes 3074 | tf_op jit(solution)/shard_map/jit(_pad)/pad | solution.py:303
  1.3 0.9 copy.12
  2.1 0.9 copy.11
  3.0 0.9 copy.13
  3.9 0.7 pad_maximum_fusion.wt_ref
  4.5 106.7 %shard_map.100 = bf16[128,128,128]{2,1,0:T(8,128)(2,1)} custom-call(bf16[128,128,128]{2,1,0:T(8,128)(2,1)} %z_hbm.1, s32[1,512]{1,0:T(1,128)} %bitcast.10, f32[1,128]{1,0:T(1,128)} %bitcast.12, f32[1,128]{1,0:T(1,128)} %bitcast.13, bf16[128,128]{1,0:T(8,128)(2,1)} %wk_ref.1, bf16[384,128]{1,0:T(8,128)(2,1)} %pad_maximum_fusion.wt_ref, ...), custom_call_target="tpu_custom_call" | custom-call | tf_op jit(solution)/shard_map/pallas_call | solution.py:286
  111.2 4.8 %copy.15 = bf16[128,128,128]{2,1,0:T(8,128)(2,1)} copy(bf16[128,128,128]{2,1,0:T(8,128)(2,1)} %shard_map.100) | data formatting | bytes 8388608

commit v3 on v2

--- a/solution.py
+++ b/solution.py
@@ -16,6 +16,7 @@
 CORES = 2
 SEND_ROWS = 2
 OUT_ROWS = 4
+SMALLS = 9
 EARLY = 4
 
 
@@ -33,11 +34,16 @@
     return op(op(t, axis=0), axis=0, keepdims=True)
 
 
-def kernel(heads, z_hbm, mask_ref, gamma_ref, beta_ref, wk_ref, wt_ref, wb_ref, wo_ref, out_hbm,
-           zbuf, own, outv, bias, btile, bsend, brow, a0, a1, k0, k1, v0, v1, q0, q1, g0, g1,
+def kernel(heads, z_hbm, *refs):
+    body(heads, z_hbm, refs[:SMALLS], refs[SMALLS + 1:2 * SMALLS + 1], refs[SMALLS], *refs[2 * SMALLS + 1:])
+
+
+def body(heads, z_hbm, small_hbm, small_refs, out_ref,
+           wt_ref, zbuf, own, outv, bias, btile, bsend, brow, a0, a1, k0, k1, v0, v1, q0, q1, g0, g1,
            s0, s1, s2, s3, go,
-           local_sem, zp_send, zp_recv, zs_send, zs_recv, b1_send, b1_recv, b2_send, b2_recv,
-           b3_send, b3_recv, o_local, o_send, o_recv):
+           small_sem, local_sem, zp_send, zp_recv, zs_send, zs_recv, b1_send, b1_recv, b2_send, b2_recv,
+           b3_send, b3_recv, o_send, o_recv):
+    mask_ref, gamma_ref, beta_ref, wq_ref, wk_ref, wv_ref, wbt_ref, wg_ref, wo_ref = small_refs
     rows_all, width, chan = z_hbm.shape
     rows = rows_all // CORES
     n_q = CORES * width
@@ -70,6 +76,13 @@
     far_at = pl.ds(pl.multiple_of((CORES + core) * width, width), width)
     z_copy = pltpu.make_async_copy(z_hbm.at[pl.ds(core * rows, rows)], zbuf.at[:, mine_at, :], local_sem.at[1])
     z_copy.start()
+    small_copies = [pltpu.make_async_copy(src, dst, small_sem.at[i]) for i, (src, dst) in enumerate(zip(small_hbm, small_refs))]
+    for c in small_copies:
+        c.start()
+    for c in small_copies:
+        c.wait()
+    for i, w in enumerate((wv_ref, wq_ref, wg_ref)):
+        wt_ref[i * proj:(i + 1) * proj] = w[...].T
     pl.semaphore_wait(barrier, len(peers))
 
     to_partner = remote(z_hbm.at[pl.ds((1 - core) * rows, rows)], zbuf.at[:, mine_at, :], zp_send, zp_recv, row, partner)
@@ -98,7 +111,7 @@
 
     def bias_step(i, carry):
         a = layer_norm(own[pl.ds(i * batch, batch)].reshape(batch * width, chan), gamma_ref[...], beta_ref[...])
-        t = lax.dot_general(wb_ref[...], a, NT, preferred_element_type=F32)
+        t = lax.dot_general(wbt_ref[...], a, NT, preferred_element_type=F32)
         for j in range(batch):
             for h in range(heads):
                 brow[h, pl.ds(i * batch + j, 1), :] = t[h:h + 1, j * width:(j + 1) * width]
@@ -176,14 +189,13 @@
         sc[h][...] = jnp.dot(k_s[slot][...], rhs, preferred_element_type=F32) + bias[h]
 
     def finish(r):
-        upd = lax.dot_general(go[...], wo_ref[...], TN, preferred_element_type=F32)
-        outv[r] = (zbuf[r, :n_q].astype(F32) + upd).astype(BF16)
-
-    def out_copies(g):
-        src = pl.ds(g * OUT_ROWS, OUT_ROWS)
-        dst = out_hbm.at[pl.ds(core * rows + g * OUT_ROWS, OUT_ROWS)]
-        return (pltpu.make_async_copy(outv.at[src, mine_at, :], dst, o_local.at[g]),
-                remote(outv.at[src, theirs_at, :], dst, o_send.at[g], o_recv.at[g], row, partner))
+        for at, dst, i in ((mine_at, out_ref, core * rows + r), (theirs_at, outv, r)):
+            upd = lax.dot_general(go[:, at], wo_ref[...], TN, preferred_element_type=F32)
+            dst[i] = (zbuf[r, at].astype(F32) + upd).astype(BF16)
+
+    def out_copy(g):
+        return remote(outv.at[pl.ds(g * OUT_ROWS, OUT_ROWS)], out_ref.at[pl.ds(core * rows + g * OUT_ROWS, OUT_ROWS)],
+                      o_send.at[g], o_recv.at[g], row, partner)
 
     def step(i, carry):
         @pl.when(i < steps - 1)
@@ -194,8 +206,7 @@
 
         @pl.when(jnp.logical_and(i >= lead, lax.rem(i - lead + OUT_ROWS, OUT_ROWS // 2) == 0))
         def _():
-            for c in out_copies((i - lead) // (OUT_ROWS // 2)):
-                c.start()
+            out_copy((i - lead) // (OUT_ROWS // 2)).start()
 
         for r in range(2):
             cur, nxt = r, 1 - r
@@ -239,8 +250,7 @@
 
     lax.fori_loop(0, steps, sent, 0)
     groups = rows // OUT_ROWS
-    for c in out_copies(groups - 1):
-        c.start()
+    out_copy(groups - 1).start()
 
     @pl.when(jnp.logical_not(home))
     def _():
@@ -257,11 +267,8 @@
             forward(t, j).wait_send()
 
     def drained(g, carry):
-        mine, theirs = out_copies(g)
-        mine.wait()
-        theirs.wait_send()
-        remote(outv.at[pl.ds(0, OUT_ROWS), theirs_at, :],
-               out_hbm.at[pl.ds((1 - core) * rows + g * OUT_ROWS, OUT_ROWS)],
+        out_copy(g).wait_send()
+        remote(outv.at[pl.ds(0, OUT_ROWS)], out_ref.at[pl.ds((1 - core) * rows + g * OUT_ROWS, OUT_ROWS)],
                o_send.at[g], o_recv.at[g], row, partner).wait_recv()
         return carry
 
@@ -282,24 +289,25 @@
         dma = pltpu.SemaphoreType.DMA
         pairs = lambda *s: [vmem(*s)] * 2
         whole = pl.BlockSpec(memory_space=pltpu.VMEM)
-        hbm = pl.BlockSpec(memory_space=pl.ANY)
+        hbm = pl.BlockSpec(memory_space=pltpu.HBM)
+        smalls = (res_mask.reshape(1, -1), ln_gamma.reshape(1, -1), ln_beta.reshape(1, -1), w_q, w_k, w_v, w_b.T, w_g, w_o)
         return pl.pallas_call(
             functools.partial(kernel, heads),
-            in_specs=[hbm] + [whole] * 7,
-            out_specs=hbm,
-            out_shape=jax.ShapeDtypeStruct(pair_tile.shape, BF16),
+            in_specs=[hbm] * (1 + len(smalls)),
+            out_specs=whole,
+            out_shape=pltpu.VMEM(pair_tile.shape, BF16),
             scratch_shapes=[
-                vmem((rows, n_k, chan), BF16), vmem((row_len, width, chan), BF16), vmem((rows, n_q, chan), BF16),
+                *[vmem(w.shape, w.dtype) for w in smalls], vmem((3 * proj, chan), BF16),
+                vmem((rows, n_k, chan), BF16), vmem((row_len, width, chan), BF16), vmem((rows, width, chan), BF16),
                 vmem((heads, n_k, n_q), F32), vmem((8, heads, width, width), BF16), vmem((heads, width, width), BF16),
                 vmem((heads, width, width), F32),
                 *pairs((n_k, chan), BF16), *pairs((n_k, proj), BF16), *pairs((proj, n_k), BF16),
                 *pairs((proj, n_q), BF16), *pairs((proj, n_q), F32),
                 *[vmem((n_k, n_q), F32)] * 4, vmem((proj, n_q), BF16),
-                dma((2,)), dma, dma, dma((CORES, steps)), dma((CORES, steps)), dma, dma, dma((2, 3)), dma((2, CORES)),
-                dma((2, CORES)), dma((2, CORES)), dma((groups,)), dma((groups,)), dma((groups,)),
+                dma((len(smalls),)), dma((2,)), dma, dma, dma((CORES, steps)), dma((CORES, steps)), dma, dma, dma((2, 3)), dma((2, CORES)),
+                dma((2, CORES)), dma((2, CORES)), dma((groups,)), dma((groups,)),
             ],
-            compiler_params=pltpu.CompilerParams(collective_id=0, has_side_effects=True, vmem_limit_bytes=56 * 1024 * 1024),
-        )(pair_tile, res_mask.reshape(1, -1), ln_gamma.reshape(1, -1), ln_beta.reshape(1, -1), w_k,
-          jnp.concatenate([w_v.T, w_q.T, w_g.T], 0), jnp.pad(w_b.T, ((0, 8 - heads), (0, 0))), w_o)
+            compiler_params=pltpu.CompilerParams(collective_id=0, has_side_effects=True, vmem_limit_bytes=58_000_000),
+        )(pair_tile, *smalls)
 
     return jax.shard_map(per_device, mesh=mesh, in_specs=(tile_spec, P('dp'), P(), P(), P(), P(), P(), P(), P(), P()), out_specs=tile_spec, check_vma=False)

time: 116 us -> 108 us (0.931)
  local copies, waits for them, and re-layouts: 8.65 us -> 2.02 us
    unnamed x4 -> x1, local copies, waits for them, and re-layouts: 7.39 us -> 2.02 us
    pad x1 -> x0, local copies, waits for them, and re-layouts: 1.26 us -> none  [per_device(): jnp.pad(w_b.T, ((0, 8 - heads), (0, 0)))]
where the time goes in v3:
time: 108 us
  Pallas kernels  106 us (98%)
  local copies, waits for them, and re-layouts  2.02 us (2%)
    pallas_call x1, Pallas kernels, per_device(): pl.pallas_call(functools.partial(kernel, heads), in_specs=[hbm] * (1 + le...  106 us

profile of v3, /device:TPU:0, one launch (start us, length us, event | category | flops | bytes accessed | tf_op | source)
XLA Modules:
  0.0 107.9 jit_solution(2840141022386886005)
XLA Ops:
  0.0 105.9 %shard_map.100 = bf16[128,128,128]{2,1,0:T(8,128)(2,1)S(1)} custom-call(bf16[128,128,128]{2,1,0:T(8,128)(2,1)} %z_hbm.1, s32[1,512]{1,0:T(1,128)} %bitcast.4, f32[1,128]{1,0:T(1,128)} %bitcast.6, f32[1,128]{1,0:T(1,128)} %bitcast.7, bf16[128,128]{1,0:T(8,128)(2,1)} %refs_3_.1, bf16[128,128]{1,0:T(8,128)(2,1)} %refs_4_.1, bf16[128,128]{1,0:T(8,128)(2,1)} %refs_5_.1, ...), custom_call_target="tpu_custom_call" | custom-call | tf_op jit(solution)/shard_map/pallas_call | solution.py:294
  105.9 2.0 %copy.12 = bf16[128,128,128]{2,1,0:T(8,128)(2,1)} copy(bf16[128,128,128]{2,1,0:T(8,128)(2,1)S(1)} %shard_map.100) | data formatting | bytes 8388608

commit v4 on v3

v4 whole, which is shorter than its diff:
```python
import functools

import jax
import jax.numpy as jnp
from jax import lax
from jax.experimental import pallas as pl
from jax.experimental.pallas import tpu as pltpu
from jax.sharding import PartitionSpec as P

LN_EPS = 1e-5
F32 = jnp.float32
BF16 = jnp.bfloat16
NT = (((1,), (1,)), ((), ()))
TN = (((0,), (0,)), ((), ()))
LOG2E = 1.4426950408889634
CORES = 2
STEP_ROWS = 2
LAST_ROWS = 10
SMALLS = 9
EARLY = 10


def layer_norm(z, gamma, beta):
    x = z.astype(F32)
    centered = x - jnp.mean(x, axis=-1, keepdims=True)
    var = jnp.mean(jnp.square(centered), axis=-1, keepdims=True)
    return (centered * lax.rsqrt(var + LN_EPS) * gamma + beta).astype(BF16)


def over_keys(x, op):
    n, width = x.shape
    groups = 8
    t = op(x.reshape(groups, n // 8 // groups, 8, width), axis=1)
    return op(op(t, axis=0), axis=0, keepdims=True)


def kernel(heads, z_hbm, *refs):
    body(heads, z_hbm, refs[:SMALLS], refs[SMALLS + 1:2 * SMALLS + 1], refs[SMALLS], *refs[2 * SMALLS + 1:])


def body(heads, z_hbm, small_hbm, small_refs, out_ref,
           wt_ref, zbuf, own, outv, bias, btile, bsend, relay, brow, a0, a1, k0, k1, v0, v1, q0, q1, g0, g1,
           s0, s1, s2, s3, go,
           small_sem, local_sem, zp_send, zp_recv, zs_send, zs_recv, b1_send, b1_recv, b2_send, b2_recv,
           b3_send, b3_recv, o_send, o_recv):
    mask_ref, gamma_ref, beta_ref, wq_ref, wk_ref, wv_ref, wbt_ref, wg_ref, wo_ref = small_refs
    rows_all, width, chan = z_hbm.shape
    rows = rows_all // CORES
    n_q = CORES * width
    proj = wk_ref.shape[1]
    hd = proj // heads
    steps = (rows - LAST_ROWS) // STEP_ROWS
    dp, row, col = lax.axis_index('dp'), lax.axis_index('row'), lax.axis_index('col')
    n_row = lax.axis_size('row')
    core, chip = lax.rem(col, CORES), col // CORES
    partner = chip * CORES + 1 - core
    far = (1 - chip) * CORES
    home_chip = row // CORES
    jslot = lax.rem(row, CORES)
    home = chip == home_chip

    def remote(src, dst, send, recv, r, c):
        return pltpu.make_async_remote_copy(src, dst, send, recv, device_id=(dp, r, c),
                                            device_id_type=pl.DeviceIdType.MESH)

    barrier = pltpu.get_barrier_semaphore()
    peers = [(row, partner), (row, far), (row, far + 1)]
    peers += [(lax.rem(row + d, n_row), col) for d in range(1, 4)]
    for r, c in peers:
        pl.semaphore_signal(barrier, inc=1, device_id=(dp, r, c), device_id_type=pl.DeviceIdType.MESH)

    own_copy = pltpu.make_async_copy(z_hbm, own, local_sem.at[0])
    own_copy.start()
    mine_at = pl.ds(pl.multiple_of(core * width, width), width)
    theirs_at = pl.ds(pl.multiple_of((1 - core) * width, width), width)
    far_at = pl.ds(pl.multiple_of((CORES + core) * width, width), width)
    z_copy = pltpu.make_async_copy(z_hbm.at[pl.ds(core * rows, rows)], zbuf.at[:, mine_at, :], local_sem.at[1])
    z_copy.start()
    pl.semaphore_wait(barrier, len(peers))

    to_partner = remote(z_hbm.at[pl.ds((1 - core) * rows, rows)], zbuf.at[:, mine_at, :], zp_send, zp_recv, row, partner)

    def z_send(r, k):
        return remote(z_hbm.at[k * rows + r], zbuf.at[r, far_at, :], zs_send.at[k, r], zs_recv.at[core, r], row, far + k)

    def z_wait(r):
        for k in range(CORES):
            at = pl.ds((CORES + k) * width, width)
            remote(z_hbm.at[0], zbuf.at[r, at, :], zs_send.at[k, r], zs_recv.at[k, r], row, far + k).wait_recv()

    def send_row(r, carry):
        for k in range(CORES):
            z_send(r, k).start()
        return carry

    lax.fori_loop(0, EARLY, send_row, 0)
    to_partner.start()
    small_copies = [pltpu.make_async_copy(src, dst, small_sem.at[i]) for i, (src, dst) in enumerate(zip(small_hbm, small_refs))]
    for c in small_copies:
        c.start()
    for c in small_copies:
        c.wait()
    for i, w in enumerate((wv_ref, wq_ref, wg_ref)):
        wt_ref[i * proj:(i + 1) * proj] = w[...].T

    own_copy.wait()
    batch = 8

    def bias_step(i, carry):
        a = layer_norm(own[pl.ds(i * batch, batch)].reshape(batch * width, chan), gamma_ref[...], beta_ref[...])
        t = lax.dot_general(wbt_ref[...], a, NT, preferred_element_type=F32)
        for j in range(batch):
            for h in range(heads):
                brow[h, pl.ds(i * batch + j, 1), :] = t[h:h + 1, j * width:(j + 1) * width]
        return carry

    lax.fori_loop(0, rows_all // batch, bias_step, 0)
    home_slot = core * CORES + jslot
    for h in range(heads):
        tile = brow[h].T.astype(BF16)
        bsend[h] = tile

        @pl.when(home)
        def _():
            btile[home_slot, h] = tile

    masks = []
    for s in range(2 * CORES):
        block = chip * CORES + s if s < CORES else far + s - CORES
        m = mask_ref[:, pl.ds(pl.multiple_of(block * width, width), width)]
        masks.append(jnp.broadcast_to(jnp.where(m > 0, 0.0, -1e9).astype(F32), (width, width)).T)

    paired = lax.rem(row + CORES, n_row)
    hand = remote(bsend, relay, b1_send.at[0], b1_recv.at[0], paired, col)
    cross_slot = (CORES + core) * CORES + jslot
    cross = remote(relay, btile.at[cross_slot], b1_send.at[1], b1_recv.at[1], row, far + core)

    def spread(src, slot, t, d):
        return remote(src, btile.at[slot], b2_send.at[d - 1], b2_recv.at[t, jslot], lax.rem(row + d, n_row), col)

    @pl.when(home)
    def _():
        for d in range(1, 4):
            spread(bsend, home_slot, 0, d).start()

    @pl.when(jnp.logical_not(home))
    def _():
        hand.start()

    @pl.when(home)
    def _():
        hand.wait_recv()
        cross.start()

    lax.fori_loop(EARLY, rows, send_row, 0)

    @pl.when(jnp.logical_not(home))
    def _():
        cross.wait_recv()
        for d in range(1, 4):
            spread(btile.at[cross_slot], cross_slot, 1, d).start()

    def forward(t, j):
        slot = (core + CORES * t) * CORES + j
        return remote(btile.at[slot], btile.at[slot], b3_send.at[t, j], b3_recv.at[t, j], row, partner)

    for t in range(2):
        for j in range(CORES):
            slot = (core + CORES * t) * CORES + j
            source = chip * CORES + j if t == 0 else far + j

            @pl.when(row != source)
            def _():
                remote(bsend, btile.at[slot], b1_send.at[0], b2_recv.at[t, j], row, partner).wait_recv()

            forward(t, j).start()
    for j in range(CORES):
        for t in range(2):
            slot = (1 - core + CORES * t) * CORES + j
            remote(bsend, btile.at[slot], b1_send.at[0], b3_recv.at[t, j], row, partner).wait_recv()

    for s in range(2 * CORES):
        for j in range(CORES):
            for h in range(heads):
                b = btile[s * CORES + j, h].astype(F32)
                bias[h, s * width:(s + 1) * width, j * width:(j + 1) * width] = (b + masks[s]) * LOG2E

    a_s, k_s, v_s, q_s, g_s, sc = (a0, a1), (k0, k1), (v0, v1), (q0, q1), (g0, g1), (s0, s1, s2, s3)
    scale = hd ** -0.5 * LOG2E

    def scores(slot, h):
        part = q_s[slot][h * hd:(h + 1) * hd, :]
        none = jnp.zeros_like(part)
        rhs = jnp.concatenate([part if i == h else none for i in range(heads)], axis=0)
        sc[h][...] = jnp.dot(k_s[slot][...], rhs, preferred_element_type=F32) + bias[h]

    def finish(r):
        for at, dst, i in ((mine_at, out_ref, core * rows + r), (theirs_at, outv, r)):
            upd = lax.dot_general(go[:, at], wo_ref[...], TN, preferred_element_type=F32)
            dst[i] = (zbuf[r, at].astype(F32) + upd).astype(BF16)

    def out_copy(g):
        return remote(outv.at[pl.ds(g * STEP_ROWS, STEP_ROWS)], out_ref.at[pl.ds(core * rows + g * STEP_ROWS, STEP_ROWS)],
                      o_send.at[g], o_recv.at[g], row, partner)

    def project(h, slot):
        a = a_s[slot]
        if h == 0:
            k_s[slot][...] = jnp.dot(a[...], wk_ref[...], preferred_element_type=F32).astype(BF16)
            t = lax.dot_general(wt_ref[proj:2 * proj], a[:n_q], NT, preferred_element_type=F32)
            q_s[slot][...] = (t * scale).astype(BF16)
        if h == 1:
            t = lax.dot_general(wt_ref[2 * proj:], a[:n_q], NT, preferred_element_type=F32)
            g_s[slot][...] = jax.nn.sigmoid(t)
        if h == 2:
            t = lax.dot_general(wt_ref[:proj], a[...], NT, preferred_element_type=F32)
            v_s[slot][...] = t.astype(BF16)

    def attend(h, slot):
        s = sc[h][...]
        p = jnp.exp2(s - over_keys(s, jnp.max))
        total = over_keys(p, jnp.sum)
        at = slice(h * hd, (h + 1) * hd)
        o = jnp.dot(v_s[slot][at, :], p.astype(BF16), preferred_element_type=F32)
        go[at, :] = (g_s[slot][at, :] * (o / total)).astype(BF16)

    def step(i, carry):
        @pl.when(i < steps)
        def _():
            for r in range(STEP_ROWS):
                z_wait(i * STEP_ROWS + r)

        @pl.when(i > 2)
        def _():
            out_copy(jnp.maximum(i, 3) - 3).start()

        for r in range(STEP_ROWS):
            cur, nxt = r, 1 - r
            finish(jnp.maximum(2 * i + r, 3) - 3)
            ahead = jnp.minimum(2 * i + r, steps * STEP_ROWS - 1)
            a_s[cur][...] = layer_norm(zbuf[ahead], gamma_ref[...], beta_ref[...])
            for h in range(heads):
                if h < 2:
                    scores(cur, h + 2)
                else:
                    scores(nxt, h - 2)
                project(h, nxt)
                attend(h, cur)
        return carry

    def last_row(r, carry):
        z_wait(r)

        @pl.when(lax.rem(r, STEP_ROWS) == 0)
        def _():
            out_copy(r // STEP_ROWS - 1).start()

        a_s[0][...] = layer_norm(zbuf[r], gamma_ref[...], beta_ref[...])
        project(0, 0)
        scores(0, 0)
        project(2, 0)
        scores(0, 1)
        project(1, 0)
        for h in range(heads):
            if h + 2 < heads:
                scores(0, h + 2)
            attend(h, 0)
        finish(r)
        return carry

    z_copy.wait()
    remote(z_hbm.at[pl.ds(0, rows)], zbuf.at[:, theirs_at, :], zp_send, zp_recv, row, partner).wait_recv()
    lax.fori_loop(0, steps + 1, step, 0)
    finish(steps * STEP_ROWS - 1)
    out_copy(steps - 2).start()
    lax.fori_loop(steps * STEP_ROWS, rows, last_row, 0)
    groups = rows // STEP_ROWS
    to_partner.wait_send()

    def sent(r, carry):
        for k in range(CORES):
            z_send(r, k).wait_send()
        return carry

    lax.fori_loop(0, rows, sent, 0)
    out_copy(groups - 1).start()

    @pl.when(jnp.logical_not(home))
    def _():
        hand.wait_send()
        for d in range(1, 4):
            spread(btile.at[cross_slot], cross_slot, 1, d).wait_send()

    @pl.when(home)
    def _():
        cross.wait_send()
        for d in range(1, 4):
            spread(bsend, home_slot, 0, d).wait_send()

    for j in range(CORES):
        for t in range(2):
            forward(t, j).wait_send()

    def drained(g, carry):
        out_copy(g).wait_send()
        remote(outv.at[pl.ds(0, STEP_ROWS)], out_ref.at[pl.ds((1 - core) * rows + g * STEP_ROWS, STEP_ROWS)],
               o_send.at[g], o_recv.at[g], row, partner).wait_recv()
        return carry

    lax.fori_loop(0, groups, drained, 0)


def solution(mesh):
    tile_spec = P(('dp', 'row'), 'col', None)

    def per_device(pair_tile, res_mask, ln_gamma, ln_beta, w_q, w_k, w_v, w_b, w_g, w_o):
        row_len, width, chan = pair_tile.shape
        heads, proj = w_b.shape[1], w_q.shape[1]
        hd = proj // heads
        rows, n_q = row_len // CORES, CORES * width
        n_k = mesh.shape['col'] * width
        groups = rows // STEP_ROWS
        vmem = pltpu.VMEM
        dma = pltpu.SemaphoreType.DMA
        pairs = lambda *s: [vmem(*s)] * 2
        whole = pl.BlockSpec(memory_space=pltpu.VMEM)
        hbm = pl.BlockSpec(memory_space=pltpu.HBM)
        smalls = (res_mask.reshape(1, -1), ln_gamma.reshape(1, -1), ln_beta.reshape(1, -1), w_q, w_k, w_v, w_b.T, w_g, w_o)
        return pl.pallas_call(
            functools.partial(kernel, heads),
            in_specs=[hbm] * (1 + len(smalls)),
            out_specs=whole,
            out_shape=pltpu.VMEM(pair_tile.shape, BF16),
            scratch_shapes=[
                *[vmem(w.shape, w.dtype) for w in smalls], vmem((3 * proj, chan), BF16),
                vmem((rows, n_k, chan), BF16), vmem((row_len, width, chan), BF16), vmem((rows, width, chan), BF16),
                vmem((heads, n_k, n_q), F32), vmem((8, heads, width, width), BF16), *pairs((heads, width, width), BF16),
                vmem((heads, width, width), F32),
                *pairs((n_k, chan), BF16), *pairs((n_k, proj), BF16), *pairs((proj, n_k), BF16),
                *pairs((proj, n_q), BF16), *pairs((proj, n_q), F32),
                *[vmem((n_k, n_q), F32)] * 4, vmem((proj, n_q), BF16),
                dma((len(smalls),)), dma((2,)), dma, dma, dma((CORES, rows)), dma((CORES, rows)), dma((2,)), dma((2,)), dma((3,)), dma((2, CORES)),
                dma((2, CORES)), dma((2, CORES)), dma((groups,)), dma((groups,)),
            ],
            compiler_params=pltpu.CompilerParams(collective_id=0, has_side_effects=True, vmem_limit_bytes=58_000_000),
        )(pair_tile, *smalls)

    return jax.shard_map(per_device, mesh=mesh, in_specs=(tile_spec, P('dp'), P(), P(), P(), P(), P(), P(), P(), P()), out_specs=tile_spec, check_vma=False)
```

time: 108 us -> 112 us (1.037)
  the two profiles are of different devices: /device:TPU:0 before, /device:TPU:7 now
where the time goes in v4:
time: 112 us
  Pallas kernels  110 us (98%)
  local copies, waits for them, and re-layouts  2.02 us (2%)
    pallas_call x1, Pallas kernels, per_device(): pl.pallas_call(functools.partial(kernel, heads), in_specs=[hbm] * (1 + le...  110 us

profile of v4, /device:TPU:7, one launch (start us, length us, event | category | flops | bytes accessed | tf_op | source)
XLA Modules:
  0.0 111.6 jit_solution(12340310542977009625)
XLA Ops:
  0.0 109.6 %shard_map.100 = bf16[128,128,128]{2,1,0:T(8,128)(2,1)S(1)} custom-call(bf16[128,128,128]{2,1,0:T(8,128)(2,1)} %z_hbm.1, s32[1,512]{1,0:T(1,128)} %bitcast.4, f32[1,128]{1,0:T(1,128)} %bitcast.6, f32[1,128]{1,0:T(1,128)} %bitcast.7, bf16[128,128]{1,0:T(8,128)(2,1)} %refs_3_.1, bf16[128,128]{1,0:T(8,128)(2,1)} %refs_4_.1, bf16[128,128]{1,0:T(8,128)(2,1)} %refs_5_.1, ...), custom_call_target="tpu_custom_call" | custom-call | tf_op jit(solution)/shard_map/pallas_call | solution.py:329
  109.6 2.0 %copy.12 = bf16[128,128,128]{2,1,0:T(8,128)(2,1)} copy(bf16[128,128,128]{2,1,0:T(8,128)(2,1)S(1)} %shard_map.100) | data formatting | bytes 8388608

commit v5 on v4

--- a/solution.py
+++ b/solution.py
@@ -15,9 +15,9 @@
 LOG2E = 1.4426950408889634
 CORES = 2
 STEP_ROWS = 2
-LAST_ROWS = 10
+LAST_ROWS = 4
 SMALLS = 9
-EARLY = 10
+EARLY = 7
 
 
 def layer_norm(z, gamma, beta):
@@ -40,7 +40,7 @@
 
 def body(heads, z_hbm, small_hbm, small_refs, out_ref,
            wt_ref, zbuf, own, outv, bias, btile, bsend, relay, brow, a0, a1, k0, k1, v0, v1, q0, q1, g0, g1,
-           s0, s1, s2, s3, go,
+           s0, s1, s2, s3, s4, s5, s6, s7, go0, go1,
            small_sem, local_sem, zp_send, zp_recv, zs_send, zs_recv, b1_send, b1_recv, b2_send, b2_recv,
            b3_send, b3_recv, o_send, o_recv):
     mask_ref, gamma_ref, beta_ref, wq_ref, wk_ref, wv_ref, wbt_ref, wg_ref, wo_ref = small_refs
@@ -49,6 +49,7 @@
     n_q = CORES * width
     proj = wk_ref.shape[1]
     hd = proj // heads
+    groups = rows // STEP_ROWS
     steps = (rows - LAST_ROWS) // STEP_ROWS
     dp, row, col = lax.axis_index('dp'), lax.axis_index('row'), lax.axis_index('col')
     n_row = lax.axis_size('row')
@@ -80,20 +81,23 @@
 
     to_partner = remote(z_hbm.at[pl.ds((1 - core) * rows, rows)], zbuf.at[:, mine_at, :], zp_send, zp_recv, row, partner)
 
-    def z_send(r, k):
-        return remote(z_hbm.at[k * rows + r], zbuf.at[r, far_at, :], zs_send.at[k, r], zs_recv.at[core, r], row, far + k)
-
-    def z_wait(r):
+    def z_send(g, k):
+        return remote(z_hbm.at[pl.ds(k * rows + g * STEP_ROWS, STEP_ROWS)],
+                      zbuf.at[pl.ds(g * STEP_ROWS, STEP_ROWS), far_at, :],
+                      zs_send.at[k, g], zs_recv.at[core, g], row, far + k)
+
+    def z_wait(g):
         for k in range(CORES):
             at = pl.ds((CORES + k) * width, width)
-            remote(z_hbm.at[0], zbuf.at[r, at, :], zs_send.at[k, r], zs_recv.at[k, r], row, far + k).wait_recv()
-
-    def send_row(r, carry):
+            remote(z_hbm.at[pl.ds(0, STEP_ROWS)], zbuf.at[pl.ds(g * STEP_ROWS, STEP_ROWS), at, :],
+                   zs_send.at[k, g], zs_recv.at[k, g], row, far + k).wait_recv()
+
+    def send_step(g, carry):
         for k in range(CORES):
-            z_send(r, k).start()
-        return carry
-
-    lax.fori_loop(0, EARLY, send_row, 0)
+            z_send(g, k).start()
+        return carry
+
+    lax.fori_loop(0, EARLY, send_step, 0)
     to_partner.start()
     small_copies = [pltpu.make_async_copy(src, dst, small_sem.at[i]) for i, (src, dst) in enumerate(zip(small_hbm, small_refs))]
     for c in small_copies:
@@ -152,7 +156,7 @@
         hand.wait_recv()
         cross.start()
 
-    lax.fori_loop(EARLY, rows, send_row, 0)
+    lax.fori_loop(EARLY, groups, send_step, 0)
 
     @pl.when(jnp.logical_not(home))
     def _():
@@ -185,50 +189,57 @@
                 b = btile[s * CORES + j, h].astype(F32)
                 bias[h, s * width:(s + 1) * width, j * width:(j + 1) * width] = (b + masks[s]) * LOG2E
 
-    a_s, k_s, v_s, q_s, g_s, sc = (a0, a1), (k0, k1), (v0, v1), (q0, q1), (g0, g1), (s0, s1, s2, s3)
+    a_s, k_s, v_s, q_s, g_s = (a0, a1), (k0, k1), (v0, v1), (q0, q1), (g0, g1)
+    sc, go = ((s0, s1, s2, s3), (s4, s5, s6, s7)), (go0, go1)
     scale = hd ** -0.5 * LOG2E
 
-    def scores(slot, h):
+    every, near, distant = slice(0, 2 * n_q), slice(0, n_q), slice(n_q, 2 * n_q)
+
+    def scores(slot, h, dst, keys=every):
         part = q_s[slot][h * hd:(h + 1) * hd, :]
         none = jnp.zeros_like(part)
         rhs = jnp.concatenate([part if i == h else none for i in range(heads)], axis=0)
-        sc[h][...] = jnp.dot(k_s[slot][...], rhs, preferred_element_type=F32) + bias[h]
-
-    def finish(r):
+        dst[h][keys, :] = jnp.dot(k_s[slot][keys, :], rhs, preferred_element_type=F32) + bias[h, keys, :]
+
+    def finish(r, src):
         for at, dst, i in ((mine_at, out_ref, core * rows + r), (theirs_at, outv, r)):
-            upd = lax.dot_general(go[:, at], wo_ref[...], TN, preferred_element_type=F32)
+            upd = lax.dot_general(src[:, at], wo_ref[...], TN, preferred_element_type=F32)
             dst[i] = (zbuf[r, at].astype(F32) + upd).astype(BF16)
 
     def out_copy(g):
         return remote(outv.at[pl.ds(g * STEP_ROWS, STEP_ROWS)], out_ref.at[pl.ds(core * rows + g * STEP_ROWS, STEP_ROWS)],
                       o_send.at[g], o_recv.at[g], row, partner)
 
-    def project(h, slot):
-        a = a_s[slot]
-        if h == 0:
-            k_s[slot][...] = jnp.dot(a[...], wk_ref[...], preferred_element_type=F32).astype(BF16)
-            t = lax.dot_general(wt_ref[proj:2 * proj], a[:n_q], NT, preferred_element_type=F32)
-            q_s[slot][...] = (t * scale).astype(BF16)
-        if h == 1:
-            t = lax.dot_general(wt_ref[2 * proj:], a[:n_q], NT, preferred_element_type=F32)
-            g_s[slot][...] = jax.nn.sigmoid(t)
-        if h == 2:
-            t = lax.dot_general(wt_ref[:proj], a[...], NT, preferred_element_type=F32)
-            v_s[slot][...] = t.astype(BF16)
-
-    def attend(h, slot):
-        s = sc[h][...]
+    def norm(r, slot, keys=every):
+        a_s[slot][keys, :] = layer_norm(zbuf[r, keys, :], gamma_ref[...], beta_ref[...])
+
+    def keys_of(slot, keys=every):
+        k_s[slot][keys, :] = jnp.dot(a_s[slot][keys, :], wk_ref[...], preferred_element_type=F32).astype(BF16)
+
+    def values_of(slot, keys=every):
+        t = lax.dot_general(wt_ref[:proj], a_s[slot][keys, :], NT, preferred_element_type=F32)
+        v_s[slot][:, keys] = t.astype(BF16)
+
+    def queries_of(slot):
+        t = lax.dot_general(wt_ref[proj:2 * proj], a_s[slot][near, :], NT, preferred_element_type=F32)
+        q_s[slot][...] = (t * scale).astype(BF16)
+
+    def gates_of(slot):
+        t = lax.dot_general(wt_ref[2 * proj:], a_s[slot][near, :], NT, preferred_element_type=F32)
+        g_s[slot][...] = jax.nn.sigmoid(t)
+
+    def attend(h, slot, src, dst):
+        s = src[h][...]
         p = jnp.exp2(s - over_keys(s, jnp.max))
         total = over_keys(p, jnp.sum)
         at = slice(h * hd, (h + 1) * hd)
         o = jnp.dot(v_s[slot][at, :], p.astype(BF16), preferred_element_type=F32)
-        go[at, :] = (g_s[slot][at, :] * (o / total)).astype(BF16)
+        dst[at, :] = (g_s[slot][at, :] * (o / total)).astype(BF16)
 
     def step(i, carry):
         @pl.when(i < steps)
         def _():
-            for r in range(STEP_ROWS):
-                z_wait(i * STEP_ROWS + r)
+            z_wait(i)
 
         @pl.when(i > 2)
         def _():
@@ -236,53 +247,68 @@
 
         for r in range(STEP_ROWS):
             cur, nxt = r, 1 - r
-            finish(jnp.maximum(2 * i + r, 3) - 3)
-            ahead = jnp.minimum(2 * i + r, steps * STEP_ROWS - 1)
-            a_s[cur][...] = layer_norm(zbuf[ahead], gamma_ref[...], beta_ref[...])
+            finish(jnp.maximum(2 * i + r, 3) - 3, go[0])
+            norm(jnp.minimum(2 * i + r, steps * STEP_ROWS - 1), cur)
             for h in range(heads):
                 if h < 2:
-                    scores(cur, h + 2)
+                    scores(cur, h + 2, sc[0])
                 else:
-                    scores(nxt, h - 2)
-                project(h, nxt)
-                attend(h, cur)
-        return carry
-
-    def last_row(r, carry):
-        z_wait(r)
-
-        @pl.when(lax.rem(r, STEP_ROWS) == 0)
-        def _():
-            out_copy(r // STEP_ROWS - 1).start()
-
-        a_s[0][...] = layer_norm(zbuf[r], gamma_ref[...], beta_ref[...])
-        project(0, 0)
-        scores(0, 0)
-        project(2, 0)
-        scores(0, 1)
-        project(1, 0)
-        for h in range(heads):
-            if h + 2 < heads:
-                scores(0, h + 2)
-            attend(h, 0)
-        finish(r)
+                    scores(nxt, h - 2, sc[0])
+                if h == 0:
+                    keys_of(nxt)
+                    queries_of(nxt)
+                if h == 1:
+                    gates_of(nxt)
+                if h == 2:
+                    values_of(nxt)
+                attend(h, cur, sc[0], go[0])
+        return carry
+
+    def last_rows(i, carry):
+        both = range(STEP_ROWS)
+        units = [(r, h) for r in both for h in range(heads)]
+        out_copy(i - 1).start()
+        for r in both:
+            norm(i * STEP_ROWS + r, r, near)
+        for r in both:
+            keys_of(r, near)
+            queries_of(r)
+            gates_of(r)
+            values_of(r, near)
+        for r, h in units:
+            scores(r, h, sc[r], near)
+        z_wait(i)
+        for r in both:
+            norm(i * STEP_ROWS + r, r, distant)
+        for r in both:
+            keys_of(r, distant)
+        ahead = 2
+        for r, h in units[:ahead]:
+            scores(r, h, sc[r], distant)
+        for r in both:
+            values_of(r, distant)
+        for n, (r, h) in enumerate(units):
+            for r2, h2 in units[n + ahead:n + ahead + 1]:
+                scores(r2, h2, sc[r2], distant)
+            attend(h, r, sc[r], go[r])
+        for r in both:
+            finish(i * STEP_ROWS + r, go[r])
         return carry
 
     z_copy.wait()
     remote(z_hbm.at[pl.ds(0, rows)], zbuf.at[:, theirs_at, :], zp_send, zp_recv, row, partner).wait_recv()
     lax.fori_loop(0, steps + 1, step, 0)
-    finish(steps * STEP_ROWS - 1)
+    finish(steps * STEP_ROWS - 1, go[0])
     out_copy(steps - 2).start()
-    lax.fori_loop(steps * STEP_ROWS, rows, last_row, 0)
-    groups = rows // STEP_ROWS
+    lax.fori_loop(steps, groups, last_rows, 0)
     to_partner.wait_send()
 
-    def sent(r, carry):
+    def sent(g, carry):
         for k in range(CORES):
-            z_send(r, k).wait_send()
-        return carry
-
-    lax.fori_loop(0, rows, sent, 0)
+            z_send(g, k).wait_send()
+        return carry
+
+    lax.fori_loop(0, groups, sent, 0)
     out_copy(groups - 1).start()
 
     @pl.when(jnp.logical_not(home))
@@ -338,8 +364,8 @@
                 vmem((heads, width, width), F32),
                 *pairs((n_k, chan), BF16), *pairs((n_k, proj), BF16), *pairs((proj, n_k), BF16),
                 *pairs((proj, n_q), BF16), *pairs((proj, n_q), F32),
-                *[vmem((n_k, n_q), F32)] * 4, vmem((proj, n_q), BF16),
-                dma((len(smalls),)), dma((2,)), dma, dma, dma((CORES, rows)), dma((CORES, rows)), dma((2,)), dma((2,)), dma((3,)), dma((2, CORES)),
+                *[vmem((n_k, n_q), F32)] * 8, *pairs((proj, n_q), BF16),
+                dma((len(smalls),)), dma((2,)), dma, dma, dma((CORES, groups)), dma((CORES, groups)), dma((2,)), dma((2,)), dma((3,)), dma((2, CORES)),
                 dma((2, CORES)), dma((2, CORES)), dma((groups,)), dma((groups,)),
             ],
             compiler_params=pltpu.CompilerParams(collective_id=0, has_side_effects=True, vmem_limit_bytes=58_000_000),

time: 112 us -> 107 us (0.955)
  the two profiles are of different devices: /device:TPU:7 before, /device:TPU:0 now
where the time goes in v5:
time: 107 us; the launch traced here: 106 us
  Pallas kernels  104 us (97%)
  local copies, waits for them, and re-layouts  2.02 us (2%)
    pallas_call x1, Pallas kernels, per_device(): pl.pallas_call(functools.partial(kernel, heads), in_specs=[hbm] * (1 + le...  104 us

profile of v5, /device:TPU:0, one launch (start us, length us, event | category | flops | bytes accessed | tf_op | source)
XLA Modules:
  0.0 106.0 jit_solution(6351408870151272394)
XLA Ops:
  0.0 104.0 %shard_map.100 = bf16[128,128,128]{2,1,0:T(8,128)(2,1)S(1)} custom-call(bf16[128,128,128]{2,1,0:T(8,128)(2,1)} %z_hbm.1, s32[1,512]{1,0:T(1,128)} %bitcast.4, f32[1,128]{1,0:T(1,128)} %bitcast.6, f32[1,128]{1,0:T(1,128)} %bitcast.7, bf16[128,128]{1,0:T(8,128)(2,1)} %refs_3_.1, bf16[128,128]{1,0:T(8,128)(2,1)} %refs_4_.1, bf16[128,128]{1,0:T(8,128)(2,1)} %refs_5_.1, ...), custom_call_target="tpu_custom_call" | custom-call | tf_op jit(solution)/shard_map/pallas_call | solution.py:355
  104.0 2.0 %copy.12 = bf16[128,128,128]{2,1,0:T(8,128)(2,1)} copy(bf16[128,128,128]{2,1,0:T(8,128)(2,1)S(1)} %shard_map.100) | data formatting | bytes 8388608

commit v6 on v5

--- a/solution.py
+++ b/solution.py
@@ -17,7 +17,8 @@
 STEP_ROWS = 2
 LAST_ROWS = 4
 SMALLS = 9
-EARLY = 7
+LAG = 6
+EARLY = 8
 
 
 def layer_norm(z, gamma, beta):
@@ -74,23 +75,30 @@
     own_copy.start()
     mine_at = pl.ds(pl.multiple_of(core * width, width), width)
     theirs_at = pl.ds(pl.multiple_of((1 - core) * width, width), width)
-    far_at = pl.ds(pl.multiple_of((CORES + core) * width, width), width)
     z_copy = pltpu.make_async_copy(z_hbm.at[pl.ds(core * rows, rows)], zbuf.at[:, mine_at, :], local_sem.at[1])
     z_copy.start()
     pl.semaphore_wait(barrier, len(peers))
 
     to_partner = remote(z_hbm.at[pl.ds((1 - core) * rows, rows)], zbuf.at[:, mine_at, :], zp_send, zp_recv, row, partner)
 
+    def z_copy_of(r, n, i, k, slot, c):
+        at = pl.ds(pl.multiple_of((CORES + slot) * width, width), width)
+        return remote(z_hbm.at[pl.ds(k * rows + r, n)], zbuf.at[pl.ds(r, n), at, :], zs_send.at[k, i], zs_recv.at[slot, i],
+                      row, far + c)
+
     def z_send(g, k):
-        return remote(z_hbm.at[pl.ds(k * rows + g * STEP_ROWS, STEP_ROWS)],
-                      zbuf.at[pl.ds(g * STEP_ROWS, STEP_ROWS), far_at, :],
-                      zs_send.at[k, g], zs_recv.at[core, g], row, far + k)
+        return z_copy_of(g * STEP_ROWS, STEP_ROWS, g, k, core, k)
+
+    def z_send_last(r, k):
+        return z_copy_of(steps * STEP_ROWS + r, 1, steps + r, k, core, k)
 
     def z_wait(g):
         for k in range(CORES):
-            at = pl.ds((CORES + k) * width, width)
-            remote(z_hbm.at[pl.ds(0, STEP_ROWS)], zbuf.at[pl.ds(g * STEP_ROWS, STEP_ROWS), at, :],
-                   zs_send.at[k, g], zs_recv.at[k, g], row, far + k).wait_recv()
+            z_copy_of(g * STEP_ROWS, STEP_ROWS, g, k, k, k).wait_recv()
+
+    def z_wait_last(r):
+        for k in range(CORES):
+            z_copy_of(steps * STEP_ROWS + r, 1, steps + r, k, k, k).wait_recv()
 
     def send_step(g, carry):
         for k in range(CORES):
@@ -139,26 +147,39 @@
     cross_slot = (CORES + core) * CORES + jslot
     cross = remote(relay, btile.at[cross_slot], b1_send.at[1], b1_recv.at[1], row, far + core)
 
+    direct = remote(bsend, btile.at[cross_slot], b1_send.at[1], b1_recv.at[1], row, far + core)
+    detour_out = jnp.logical_or(chip == 1, core == 1)
+    detour_in = jnp.logical_or(chip == 0, core == 1)
+    away = jnp.logical_not(home)
+    lands = jnp.logical_or(jnp.logical_and(detour_in, away), jnp.logical_and(jnp.logical_not(detour_in), home))
+
     def spread(src, slot, t, d):
-        return remote(src, btile.at[slot], b2_send.at[d - 1], b2_recv.at[t, jslot], lax.rem(row + d, n_row), col)
+        return remote(src, btile.at[slot], b2_send.at[t, d - 1], b2_recv.at[t, jslot], lax.rem(row + d, n_row), col)
+
+    @pl.when(jnp.logical_and(away, detour_out))
+    def _():
+        hand.start()
+
+    @pl.when(jnp.logical_and(away, jnp.logical_not(detour_out)))
+    def _():
+        direct.start()
 
     @pl.when(home)
     def _():
         for d in range(1, 4):
             spread(bsend, home_slot, 0, d).start()
 
-    @pl.when(jnp.logical_not(home))
-    def _():
-        hand.start()
-
-    @pl.when(home)
+    @pl.when(jnp.logical_and(home, detour_out))
     def _():
         hand.wait_recv()
         cross.start()
 
-    lax.fori_loop(EARLY, groups, send_step, 0)
-
-    @pl.when(jnp.logical_not(home))
+    lax.fori_loop(EARLY, steps, send_step, 0)
+    for r in range(LAST_ROWS):
+        for k in range(CORES):
+            z_send_last(r, k).start()
+
+    @pl.when(lands)
     def _():
         cross.wait_recv()
         for d in range(1, 4):
@@ -171,7 +192,9 @@
     for t in range(2):
         for j in range(CORES):
             slot = (core + CORES * t) * CORES + j
-            source = chip * CORES + j if t == 0 else far + j
+            source = chip * CORES + j
+            if t == 1:
+                source = jnp.where(detour_in, far + j, source)
 
             @pl.when(row != source)
             def _():
@@ -236,6 +259,17 @@
         o = jnp.dot(v_s[slot][at, :], p.astype(BF16), preferred_element_type=F32)
         dst[at, :] = (g_s[slot][at, :] * (o / total)).astype(BF16)
 
+    def sent(g, carry):
+        for k in range(CORES):
+            z_send(g, k).wait_send()
+        return carry
+
+    def drained(g, carry):
+        out_copy(g).wait_send()
+        remote(outv.at[pl.ds(0, STEP_ROWS)], out_ref.at[pl.ds((1 - core) * rows + g * STEP_ROWS, STEP_ROWS)],
+               o_send.at[g], o_recv.at[g], row, partner).wait_recv()
+        return carry
+
     def step(i, carry):
         @pl.when(i < steps)
         def _():
@@ -244,6 +278,12 @@
         @pl.when(i > 2)
         def _():
             out_copy(jnp.maximum(i, 3) - 3).start()
+
+        @pl.when(i >= LAG)
+        def _():
+            g = jnp.maximum(i, LAG) - LAG
+            sent(g, 0)
+            drained(g, 0)
 
         for r in range(STEP_ROWS):
             cur, nxt = r, 1 - r
@@ -277,21 +317,17 @@
             values_of(r, near)
         for r, h in units:
             scores(r, h, sc[r], near)
-        z_wait(i)
         for r in both:
+            z_wait_last((i - steps) * STEP_ROWS + r)
             norm(i * STEP_ROWS + r, r, distant)
-        for r in both:
             keys_of(r, distant)
-        ahead = 2
-        for r, h in units[:ahead]:
-            scores(r, h, sc[r], distant)
-        for r in both:
+            scores(r, 0, sc[r], distant)
+            scores(r, 1, sc[r], distant)
             values_of(r, distant)
-        for n, (r, h) in enumerate(units):
-            for r2, h2 in units[n + ahead:n + ahead + 1]:
-                scores(r2, h2, sc[r2], distant)
-            attend(h, r, sc[r], go[r])
-        for r in both:
+            for h in range(heads):
+                if h + 2 < heads:
+                    scores(r, h + 2, sc[r], distant)
+                attend(h, r, sc[r], go[r])
             finish(i * STEP_ROWS + r, go[r])
         return carry
 
@@ -302,38 +338,35 @@
     out_copy(steps - 2).start()
     lax.fori_loop(steps, groups, last_rows, 0)
     to_partner.wait_send()
-
-    def sent(g, carry):
-        for k in range(CORES):
-            z_send(g, k).wait_send()
-        return carry
-
-    lax.fori_loop(0, groups, sent, 0)
+    lax.fori_loop(steps + 1 - LAG, steps, sent, 0)
+    for r in range(LAST_ROWS):
+        for k in range(CORES):
+            z_send_last(r, k).wait_send()
     out_copy(groups - 1).start()
 
-    @pl.when(jnp.logical_not(home))
+    @pl.when(jnp.logical_and(away, detour_out))
     def _():
         hand.wait_send()
+
+    @pl.when(jnp.logical_or(jnp.logical_and(home, detour_out), jnp.logical_and(away, jnp.logical_not(detour_out))))
+    def _():
+        cross.wait_send()
+
+    @pl.when(home)
+    def _():
+        for d in range(1, 4):
+            spread(bsend, home_slot, 0, d).wait_send()
+
+    @pl.when(lands)
+    def _():
         for d in range(1, 4):
             spread(btile.at[cross_slot], cross_slot, 1, d).wait_send()
-
-    @pl.when(home)
-    def _():
-        cross.wait_send()
-        for d in range(1, 4):
-            spread(bsend, home_slot, 0, d).wait_send()
 
     for j in range(CORES):
         for t in range(2):
             forward(t, j).wait_send()
 
-    def drained(g, carry):
-        out_copy(g).wait_send()
-        remote(outv.at[pl.ds(0, STEP_ROWS)], out_ref.at[pl.ds((1 - core) * rows + g * STEP_ROWS, STEP_ROWS)],
-               o_send.at[g], o_recv.at[g], row, partner).wait_recv()
-        return carry
-
-    lax.fori_loop(0, groups, drained, 0)
+    lax.fori_loop(steps + 1 - LAG, groups, drained, 0)
 
 
 def solution(mesh):
@@ -346,6 +379,7 @@
         rows, n_q = row_len // CORES, CORES * width
         n_k = mesh.shape['col'] * width
         groups = rows // STEP_ROWS
+        copies = (rows - LAST_ROWS) // STEP_ROWS + LAST_ROWS
         vmem = pltpu.VMEM
         dma = pltpu.SemaphoreType.DMA
         pairs = lambda *s: [vmem(*s)] * 2
@@ -365,7 +399,7 @@
                 *pairs((n_k, chan), BF16), *pairs((n_k, proj), BF16), *pairs((proj, n_k), BF16),
                 *pairs((proj, n_q), BF16), *pairs((proj, n_q), F32),
                 *[vmem((n_k, n_q), F32)] * 8, *pairs((proj, n_q), BF16),
-                dma((len(smalls),)), dma((2,)), dma, dma, dma((CORES, groups)), dma((CORES, groups)), dma((2,)), dma((2,)), dma((3,)), dma((2, CORES)),
+                dma((len(smalls),)), dma((2,)), dma, dma, dma((CORES, copies)), dma((CORES, copies)), dma((2,)), dma((2,)), dma((2, 3)), dma((2, CORES)),
                 dma((2, CORES)), dma((2, CORES)), dma((groups,)), dma((groups,)),
             ],
             compiler_params=pltpu.CompilerParams(collective_id=0, has_side_effects=True, vmem_limit_bytes=58_000_000),

time: 107 us -> 108 us (level)
  Pallas kernels: 104 us -> 106 us
    pallas_call x1, Pallas kernels: 104 us -> 106 us  [per_device(): pl.pallas_call(functools.partial(kernel, heads), in_specs=[hbm] * (1 + le...]
where the time goes in v6:
time: 108 us
  Pallas kernels  106 us (98%)
  local copies, waits for them, and re-layouts  2.02 us (2%)
    pallas_call x1, Pallas kernels, per_device(): pl.pallas_call(functools.partial(kernel, heads), in_specs=[hbm] * (1 + le...  106 us

profile of v6, /device:TPU:0, one launch (start us, length us, event | category | flops | bytes accessed | tf_op | source)
XLA Modules:
  0.0 107.7 jit_solution(7186973429414526749)
XLA Ops:
  0.0 105.6 %shard_map.100 = bf16[128,128,128]{2,1,0:T(8,128)(2,1)S(1)} custom-call(bf16[128,128,128]{2,1,0:T(8,128)(2,1)} %z_hbm.1, s32[1,512]{1,0:T(1,128)} %bitcast.4, f32[1,128]{1,0:T(1,128)} %bitcast.6, f32[1,128]{1,0:T(1,128)} %bitcast.7, bf16[128,128]{1,0:T(8,128)(2,1)} %refs_3_.1, bf16[128,128]{1,0:T(8,128)(2,1)} %refs_4_.1, bf16[128,128]{1,0:T(8,128)(2,1)} %refs_5_.1, ...), custom_call_target="tpu_custom_call" | custom-call | tf_op jit(solution)/shard_map/pallas_call | solution.py:389
  105.7 2.0 %copy.12 = bf16[128,128,128]{2,1,0:T(8,128)(2,1)} copy(bf16[128,128,128]{2,1,0:T(8,128)(2,1)S(1)} %shard_map.100) | data formatting | bytes 8388608

commit v7 on v6

--- a/solution.py
+++ b/solution.py
@@ -18,7 +18,7 @@
 LAST_ROWS = 4
 SMALLS = 9
 LAG = 6
-EARLY = 8
+EARLY = 5
 
 
 def layer_norm(z, gamma, beta):
@@ -81,24 +81,17 @@
 
     to_partner = remote(z_hbm.at[pl.ds((1 - core) * rows, rows)], zbuf.at[:, mine_at, :], zp_send, zp_recv, row, partner)
 
-    def z_copy_of(r, n, i, k, slot, c):
+    def z_copy_of(g, k, slot, c):
         at = pl.ds(pl.multiple_of((CORES + slot) * width, width), width)
-        return remote(z_hbm.at[pl.ds(k * rows + r, n)], zbuf.at[pl.ds(r, n), at, :], zs_send.at[k, i], zs_recv.at[slot, i],
-                      row, far + c)
+        return remote(z_hbm.at[pl.ds(k * rows + g * STEP_ROWS, STEP_ROWS)],
+                      zbuf.at[pl.ds(g * STEP_ROWS, STEP_ROWS), at, :], zs_send.at[k, g], zs_recv.at[slot, g], row, far + c)
 
     def z_send(g, k):
-        return z_copy_of(g * STEP_ROWS, STEP_ROWS, g, k, core, k)
-
-    def z_send_last(r, k):
-        return z_copy_of(steps * STEP_ROWS + r, 1, steps + r, k, core, k)
+        return z_copy_of(g, k, core, k)
 
     def z_wait(g):
         for k in range(CORES):
-            z_copy_of(g * STEP_ROWS, STEP_ROWS, g, k, k, k).wait_recv()
-
-    def z_wait_last(r):
-        for k in range(CORES):
-            z_copy_of(steps * STEP_ROWS + r, 1, steps + r, k, k, k).wait_recv()
+            z_copy_of(g, k, k, k).wait_recv()
 
     def send_step(g, carry):
         for k in range(CORES):
@@ -116,10 +109,14 @@
         wt_ref[i * proj:(i + 1) * proj] = w[...].T
 
     own_copy.wait()
-    batch = 8
+    batch = 16
+    mean_of = jnp.full((chan, chan), 1 / chan, BF16)
 
     def bias_step(i, carry):
-        a = layer_norm(own[pl.ds(i * batch, batch)].reshape(batch * width, chan), gamma_ref[...], beta_ref[...])
+        z = own[pl.ds(i * batch, batch)].reshape(batch * width, chan)
+        centered = z.astype(F32) - jnp.dot(z, mean_of, preferred_element_type=F32)
+        var = jnp.mean(jnp.square(centered), axis=-1, keepdims=True)
+        a = (centered * lax.rsqrt(var + LN_EPS) * gamma_ref[...] + beta_ref[...]).astype(BF16)
         t = lax.dot_general(wbt_ref[...], a, NT, preferred_element_type=F32)
         for j in range(batch):
             for h in range(heads):
@@ -174,10 +171,7 @@
         hand.wait_recv()
         cross.start()
 
-    lax.fori_loop(EARLY, steps, send_step, 0)
-    for r in range(LAST_ROWS):
-        for k in range(CORES):
-            z_send_last(r, k).start()
+    lax.fori_loop(EARLY, groups, send_step, 0)
 
     @pl.when(lands)
     def _():
@@ -278,12 +272,6 @@
         @pl.when(i > 2)
         def _():
             out_copy(jnp.maximum(i, 3) - 3).start()
-
-        @pl.when(i >= LAG)
-        def _():
-            g = jnp.maximum(i, LAG) - LAG
-            sent(g, 0)
-            drained(g, 0)
 
         for r in range(STEP_ROWS):
             cur, nxt = r, 1 - r
@@ -317,17 +305,21 @@
             values_of(r, near)
         for r, h in units:
             scores(r, h, sc[r], near)
-        for r in both:
-            z_wait_last((i - steps) * STEP_ROWS + r)
+        z_wait(i)
+        for r in both:
             norm(i * STEP_ROWS + r, r, distant)
+        for r in both:
             keys_of(r, distant)
-            scores(r, 0, sc[r], distant)
-            scores(r, 1, sc[r], distant)
+        ahead = 2
+        for r, h in units[:ahead]:
+            scores(r, h, sc[r], distant)
+        for r in both:
             values_of(r, distant)
-            for h in range(heads):
-                if h + 2 < heads:
-                    scores(r, h + 2, sc[r], distant)
-                attend(h, r, sc[r], go[r])
+        for n, (r, h) in enumerate(units):
+            for r2, h2 in units[n + ahead:n + ahead + 1]:
+                scores(r2, h2, sc[r2], distant)
+            attend(h, r, sc[r], go[r])
+        for r in both:
             finish(i * STEP_ROWS + r, go[r])
         return carry
 
@@ -336,12 +328,11 @@
     lax.fori_loop(0, steps + 1, step, 0)
     finish(steps * STEP_ROWS - 1, go[0])
     out_copy(steps - 2).start()
+    lax.fori_loop(0, steps + 1 - LAG, sent, 0)
+    lax.fori_loop(0, steps + 1 - LAG, drained, 0)
     lax.fori_loop(steps, groups, last_rows, 0)
     to_partner.wait_send()
-    lax.fori_loop(steps + 1 - LAG, steps, sent, 0)
-    for r in range(LAST_ROWS):
-        for k in range(CORES):
-            z_send_last(r, k).wait_send()
+    lax.fori_loop(steps + 1 - LAG, groups, sent, 0)
     out_copy(groups - 1).start()
 
     @pl.when(jnp.logical_and(away, detour_out))
@@ -379,7 +370,6 @@
         rows, n_q = row_len // CORES, CORES * width
         n_k = mesh.shape['col'] * width
         groups = rows // STEP_ROWS
-        copies = (rows - LAST_ROWS) // STEP_ROWS + LAST_ROWS
         vmem = pltpu.VMEM
         dma = pltpu.SemaphoreType.DMA
         pairs = lambda *s: [vmem(*s)] * 2
@@ -399,7 +389,7 @@
                 *pairs((n_k, chan), BF16), *pairs((n_k, proj), BF16), *pairs((proj, n_k), BF16),
                 *pairs((proj, n_q), BF16), *pairs((proj, n_q), F32),
                 *[vmem((n_k, n_q), F32)] * 8, *pairs((proj, n_q), BF16),
-                dma((len(smalls),)), dma((2,)), dma, dma, dma((CORES, copies)), dma((CORES, copies)), dma((2,)), dma((2,)), dma((2, 3)), dma((2, CORES)),
+                dma((len(smalls),)), dma((2,)), dma, dma, dma((CORES, groups)), dma((CORES, groups)), dma((2,)), dma((2,)), dma((2, 3)), dma((2, CORES)),
                 dma((2, CORES)), dma((2, CORES)), dma((groups,)), dma((groups,)),
             ],
             compiler_params=pltpu.CompilerParams(collective_id=0, has_side_effects=True, vmem_limit_bytes=58_000_000),

time: 108 us -> 107 us (level)
  Pallas kernels: 106 us -> 104 us
    pallas_call x1, Pallas kernels: 106 us -> 104 us  [per_device(): pl.pallas_call(functools.partial(kernel, heads), in_specs=[hbm] * (1 + le...]
where the time goes in v7:
time: 107 us; the launch traced here: 106 us
  Pallas kernels  104 us (97%)
  local copies, waits for them, and re-layouts  2.02 us (2%)
    pallas_call x1, Pallas kernels, per_device(): pl.pallas_call(functools.partial(kernel, heads), in_specs=[hbm] * (1 + le...  104 us

profile of v7, /device:TPU:0, one launch (start us, length us, event | category | flops | bytes accessed | tf_op | source)
XLA Modules:
  0.0 106.3 jit_solution(12582090639282417038)
XLA Ops:
  0.0 104.2 %shard_map.100 = bf16[128,128,128]{2,1,0:T(8,128)(2,1)S(1)} custom-call(bf16[128,128,128]{2,1,0:T(8,128)(2,1)} %z_hbm.1, s32[1,512]{1,0:T(1,128)} %bitcast.4, f32[1,128]{1,0:T(1,128)} %bitcast.6, f32[1,128]{1,0:T(1,128)} %bitcast.7, bf16[128,128]{1,0:T(8,128)(2,1)} %refs_3_.1, bf16[128,128]{1,0:T(8,128)(2,1)} %refs_4_.1, bf16[128,128]{1,0:T(8,128)(2,1)} %refs_5_.1, ...), custom_call_target="tpu_custom_call" | custom-call | tf_op jit(solution)/shard_map/pallas_call | solution.py:379
  104.2 2.0 %copy.12 = bf16[128,128,128]{2,1,0:T(8,128)(2,1)} copy(bf16[128,128,128]{2,1,0:T(8,128)(2,1)S(1)} %shard_map.100) | data formatting | bytes 8388608

commit v8 on v7

--- a/solution.py
+++ b/solution.py
@@ -15,10 +15,12 @@
 LOG2E = 1.4426950408889634
 CORES = 2
 STEP_ROWS = 2
+BIG = 2
+SMALL_ROWS = 8
 LAST_ROWS = 4
 SMALLS = 9
 LAG = 6
-EARLY = 5
+EARLY = 3
 
 
 def layer_norm(z, gamma, beta):
@@ -81,22 +83,35 @@
 
     to_partner = remote(z_hbm.at[pl.ds((1 - core) * rows, rows)], zbuf.at[:, mine_at, :], zp_send, zp_recv, row, partner)
 
-    def z_copy_of(g, k, slot, c):
+    bigs = (rows - SMALL_ROWS) // (BIG * STEP_ROWS)
+
+    def z_copy_of(i, n, at_row, k, slot, c):
         at = pl.ds(pl.multiple_of((CORES + slot) * width, width), width)
-        return remote(z_hbm.at[pl.ds(k * rows + g * STEP_ROWS, STEP_ROWS)],
-                      zbuf.at[pl.ds(g * STEP_ROWS, STEP_ROWS), at, :], zs_send.at[k, g], zs_recv.at[slot, g], row, far + c)
-
-    def z_send(g, k):
-        return z_copy_of(g, k, core, k)
+        return remote(z_hbm.at[pl.ds(k * rows + at_row, n)], zbuf.at[pl.ds(at_row, n), at, :],
+                      zs_send.at[k, i], zs_recv.at[slot, i], row, far + c)
+
+    def big(i, k, slot):
+        n = BIG * STEP_ROWS
+        return z_copy_of(i, n, i * n, k, slot, k)
+
+    def small(g, k, slot):
+        return z_copy_of(bigs + g - bigs * BIG, STEP_ROWS, g * STEP_ROWS, k, slot, k)
+
+    def send_step(i, carry):
+        for k in range(CORES):
+            big(i, k, core).start()
+        return carry
 
     def z_wait(g):
-        for k in range(CORES):
-            z_copy_of(g, k, k, k).wait_recv()
-
-    def send_step(g, carry):
-        for k in range(CORES):
-            z_send(g, k).start()
-        return carry
+        @pl.when(jnp.logical_and(g < bigs * BIG, lax.rem(g, BIG) == 0))
+        def _():
+            for k in range(CORES):
+                big(jnp.minimum(g, bigs * BIG - 1) // BIG, k, k).wait_recv()
+
+        @pl.when(g >= bigs * BIG)
+        def _():
+            for k in range(CORES):
+                small(jnp.maximum(g, bigs * BIG), k, k).wait_recv()
 
     lax.fori_loop(0, EARLY, send_step, 0)
     to_partner.start()
@@ -171,7 +186,10 @@
         hand.wait_recv()
         cross.start()
 
-    lax.fori_loop(EARLY, groups, send_step, 0)
+    lax.fori_loop(EARLY, bigs, send_step, 0)
+    for g in range(bigs * BIG, groups):
+        for k in range(CORES):
+            small(g, k, core).start()
 
     @pl.when(lands)
     def _():
@@ -253,9 +271,9 @@
         o = jnp.dot(v_s[slot][at, :], p.astype(BF16), preferred_element_type=F32)
         dst[at, :] = (g_s[slot][at, :] * (o / total)).astype(BF16)
 
-    def sent(g, carry):
+    def sent(i, carry):
         for k in range(CORES):
-            z_send(g, k).wait_send()
+            big(i, k, core).wait_send()
         return carry
 
     def drained(g, carry):
@@ -328,11 +346,14 @@
     lax.fori_loop(0, steps + 1, step, 0)
     finish(steps * STEP_ROWS - 1, go[0])
     out_copy(steps - 2).start()
-    lax.fori_loop(0, steps + 1 - LAG, sent, 0)
+    lax.fori_loop(0, bigs - LAG, sent, 0)
     lax.fori_loop(0, steps + 1 - LAG, drained, 0)
     lax.fori_loop(steps, groups, last_rows, 0)
     to_partner.wait_send()
-    lax.fori_loop(steps + 1 - LAG, groups, sent, 0)
+    lax.fori_loop(bigs - LAG, bigs, sent, 0)
+    for g in range(bigs * BIG, groups):
+        for k in range(CORES):
+            small(g, k, core).wait_send()
     out_copy(groups - 1).start()
 
     @pl.when(jnp.logical_and(away, detour_out))
@@ -358,6 +379,16 @@
             forward(t, j).wait_send()
 
     lax.fori_loop(steps + 1 - LAG, groups, drained, 0)
+
+
+def write_out(src, dst, sem):
+    parts = sem.shape[0]
+    n = src.shape[0] // parts
+    copies = [pltpu.make_async_copy(src.at[pl.ds(i * n, n)], dst.at[pl.ds(i * n, n)], sem.at[i]) for i in range(parts)]
+    for c in copies:
+        c.start()
+    for c in copies:
+        c.wait()
 
 
 def solution(mesh):
@@ -376,7 +407,7 @@
         whole = pl.BlockSpec(memory_space=pltpu.VMEM)
         hbm = pl.BlockSpec(memory_space=pltpu.HBM)
         smalls = (res_mask.reshape(1, -1), ln_gamma.reshape(1, -1), ln_beta.reshape(1, -1), w_q, w_k, w_v, w_b.T, w_g, w_o)
-        return pl.pallas_call(
+        result = pl.pallas_call(
             functools.partial(kernel, heads),
             in_specs=[hbm] * (1 + len(smalls)),
             out_specs=whole,
@@ -394,5 +425,13 @@
             ],
             compiler_params=pltpu.CompilerParams(collective_id=0, has_side_effects=True, vmem_limit_bytes=58_000_000),
         )(pair_tile, *smalls)
+        return pl.pallas_call(
+            write_out,
+            in_specs=[pl.BlockSpec(memory_space=pl.ANY)],
+            out_specs=hbm,
+            out_shape=jax.ShapeDtypeStruct(pair_tile.shape, BF16),
+            scratch_shapes=[dma((4,))],
+            compiler_params=pltpu.CompilerParams(vmem_limit_bytes=4 * 1024 * 1024),
+        )(result)
 
     return jax.shard_map(per_device, mesh=mesh, in_specs=(tile_spec, P('dp'), P(), P(), P(), P(), P(), P(), P(), P()), out_specs=tile_spec, check_vma=False)

time: 107 us -> 106 us (level)
  local copies, waits for them, and re-layouts: 2.02 us -> 0 us
  Pallas kernels: 104 us -> 106 us
    pallas_call x0 -> x1, Pallas kernels: none -> 2.04 us  [per_device(): pl.pallas_call(write_out, in_specs=[pl.BlockSpec(memory_space=pl.ANY)], o...]
    unnamed x1 -> x0, local copies, waits for them, and re-layouts: 2.02 us -> none
where the time goes in v8:
time: 106 us
  Pallas kernels  106 us (100%)
    pallas_call x1, Pallas kernels, per_device(): pl.pallas_call(functools.partial(kernel, heads), in_specs=[hbm] * (1 + le...  104 us

profile of v8, /device:TPU:0, one launch (start us, length us, event | category | flops | bytes accessed | tf_op | source)
XLA Modules:
  0.0 105.9 jit_solution(14024050516537631708)
XLA Ops:
  0.0 103.9 %shard_map.100.src = bf16[128,128,128]{2,1,0:T(8,128)(2,1)S(1)} custom-call(bf16[128,128,128]{2,1,0:T(8,128)(2,1)} %z_hbm.1, s32[1,512]{1,0:T(1,128)} %bitcast.4, f32[1,128]{1,0:T(1,128)} %bitcast.6, f32[1,128]{1,0:T(1,128)} %bitcast.7, bf16[128,128]{1,0:T(8,128)(2,1)} %refs_3_.1, bf16[128,128]{1,0:T(8,128)(2,1)} %refs_4_.1, bf16[128,128]{1,0:T(8,128)(2,1)} %refs_5_.1, ...), custom_call_target="tpu_custom_call" | custom-call | tf_op jit(solution)/shard_map/pallas_call | solution.py:410
  103.9 2.0 %shard_map.101 = bf16[128,128,128]{2,1,0:T(8,128)(2,1)} custom-call(bf16[128,128,128]{2,1,0:T(8,128)(2,1)S(1)} %shard_map.100.src), custom_call_target="tpu_custom_call" | custom-call | tf_op jit(solution)/shard_map/pallas_call | solution.py:428

commit v9 on v8

--- a/solution.py
+++ b/solution.py
@@ -44,7 +44,7 @@
 def body(heads, z_hbm, small_hbm, small_refs, out_ref,
            wt_ref, zbuf, own, outv, bias, btile, bsend, relay, brow, a0, a1, k0, k1, v0, v1, q0, q1, g0, g1,
            s0, s1, s2, s3, s4, s5, s6, s7, go0, go1,
-           small_sem, local_sem, zp_send, zp_recv, zs_send, zs_recv, b1_send, b1_recv, b2_send, b2_recv,
+           round_sem, small_sem, local_sem, zp_send, zp_recv, zs_send, zs_recv, b1_send, b1_recv, b2_send, b2_recv,
            b3_send, b3_recv, o_send, o_recv):
     mask_ref, gamma_ref, beta_ref, wq_ref, wk_ref, wv_ref, wbt_ref, wg_ref, wo_ref = small_refs
     rows_all, width, chan = z_hbm.shape
@@ -67,11 +67,24 @@
         return pltpu.make_async_remote_copy(src, dst, send, recv, device_id=(dp, r, c),
                                             device_id_type=pl.DeviceIdType.MESH)
 
+    def signal(sem, r, c):
+        pl.semaphore_signal(sem, inc=1, device_id=(dp, r, c), device_id_type=pl.DeviceIdType.MESH)
+
+    def tell_next_rows(sem):
+        @pl.when(row > 0)
+        def _():
+            signal(sem, jnp.maximum(row, 1) - 1, col)
+
+        @pl.when(row < n_row - 1)
+        def _():
+            signal(sem, jnp.minimum(row, n_row - 2) + 1, col)
+
+    next_rows = jnp.where(row > 0, 1, 0) + jnp.where(row < n_row - 1, 1, 0)
+
     barrier = pltpu.get_barrier_semaphore()
-    peers = [(row, partner), (row, far), (row, far + 1)]
-    peers += [(lax.rem(row + d, n_row), col) for d in range(1, 4)]
-    for r, c in peers:
-        pl.semaphore_signal(barrier, inc=1, device_id=(dp, r, c), device_id_type=pl.DeviceIdType.MESH)
+    for c in (partner, far, far + 1):
+        signal(barrier, row, c)
+    tell_next_rows(barrier)
 
     own_copy = pltpu.make_async_copy(z_hbm, own, local_sem.at[0])
     own_copy.start()
@@ -79,7 +92,7 @@
     theirs_at = pl.ds(pl.multiple_of((1 - core) * width, width), width)
     z_copy = pltpu.make_async_copy(z_hbm.at[pl.ds(core * rows, rows)], zbuf.at[:, mine_at, :], local_sem.at[1])
     z_copy.start()
-    pl.semaphore_wait(barrier, len(peers))
+    pl.semaphore_wait(barrier, 3 + next_rows)
 
     to_partner = remote(z_hbm.at[pl.ds((1 - core) * rows, rows)], zbuf.at[:, mine_at, :], zp_send, zp_recv, row, partner)
 
@@ -148,6 +161,10 @@
         def _():
             btile[home_slot, h] = tile
 
+    for i in range(2):
+        tell_next_rows(round_sem.at[i])
+        pl.semaphore_wait(round_sem.at[i], next_rows)
+
     masks = []
     for s in range(2 * CORES):
         block = chip * CORES + s if s < CORES else far + s - CORES
@@ -237,7 +254,7 @@
         dst[h][keys, :] = jnp.dot(k_s[slot][keys, :], rhs, preferred_element_type=F32) + bias[h, keys, :]
 
     def finish(r, src):
-        for at, dst, i in ((mine_at, out_ref, core * rows + r), (theirs_at, outv, r)):
+        for at, dst, i in ((theirs_at, outv, r), (mine_at, out_ref, core * rows + r)):
             upd = lax.dot_general(src[:, at], wo_ref[...], TN, preferred_element_type=F32)
             dst[i] = (zbuf[r, at].astype(F32) + upd).astype(BF16)
 
@@ -350,11 +367,11 @@
     lax.fori_loop(0, steps + 1 - LAG, drained, 0)
     lax.fori_loop(steps, groups, last_rows, 0)
     to_partner.wait_send()
+    out_copy(groups - 1).start()
     lax.fori_loop(bigs - LAG, bigs, sent, 0)
     for g in range(bigs * BIG, groups):
         for k in range(CORES):
             small(g, k, core).wait_send()
-    out_copy(groups - 1).start()
 
     @pl.when(jnp.logical_and(away, detour_out))
     def _():
@@ -420,7 +437,7 @@
                 *pairs((n_k, chan), BF16), *pairs((n_k, proj), BF16), *pairs((proj, n_k), BF16),
                 *pairs((proj, n_q), BF16), *pairs((proj, n_q), F32),
                 *[vmem((n_k, n_q), F32)] * 8, *pairs((proj, n_q), BF16),
-                dma((len(smalls),)), dma((2,)), dma, dma, dma((CORES, groups)), dma((CORES, groups)), dma((2,)), dma((2,)), dma((2, 3)), dma((2, CORES)),
+                pltpu.SemaphoreType.REGULAR((2,)), dma((len(smalls),)), dma((2,)), dma, dma, dma((CORES, groups)), dma((CORES, groups)), dma((2,)), dma((2,)), dma((2, 3)), dma((2, CORES)),
                 dma((2, CORES)), dma((2, CORES)), dma((groups,)), dma((groups,)),
             ],
             compiler_params=pltpu.CompilerParams(collective_id=0, has_side_effects=True, vmem_limit_bytes=58_000_000),

time: 106 us -> 106 us (level); the launches traced: 106 us -> 104 us
  Pallas kernels: 106 us -> 104 us
    pallas_call x1, Pallas kernels: 104 us -> 102 us  [per_device(): pl.pallas_call(functools.partial(kernel, heads), in_specs=[hbm] * (1 + le...]
where the time goes in v9:
time: 106 us; the launch traced here: 104 us
  Pallas kernels  104 us (98%)
    pallas_call x1, Pallas kernels, per_device(): pl.pallas_call(functools.partial(kernel, heads), in_specs=[hbm] * (1 + le...  102 us

profile of v9, /device:TPU:0, one launch (start us, length us, event | category | flops | bytes accessed | tf_op | source)
XLA Modules:
  0.0 103.9 jit_solution(9686647899780675544)
XLA Ops:
  0.0 101.8 %shard_map.100.src = bf16[128,128,128]{2,1,0:T(8,128)(2,1)S(1)} custom-call(bf16[128,128,128]{2,1,0:T(8,128)(2,1)} %z_hbm.1, s32[1,512]{1,0:T(1,128)} %bitcast.4, f32[1,128]{1,0:T(1,128)} %bitcast.6, f32[1,128]{1,0:T(1,128)} %bitcast.7, bf16[128,128]{1,0:T(8,128)(2,1)} %refs_3_.1, bf16[128,128]{1,0:T(8,128)(2,1)} %refs_4_.1, bf16[128,128]{1,0:T(8,128)(2,1)} %refs_5_.1, ...), custom_call_target="tpu_custom_call" | custom-call | tf_op jit(solution)/shard_map/pallas_call | solution.py:427
  101.8 2.0 %shard_map.101 = bf16[128,128,128]{2,1,0:T(8,128)(2,1)} custom-call(bf16[128,128,128]{2,1,0:T(8,128)(2,1)S(1)} %shard_map.100.src), custom_call_target="tpu_custom_call" | custom-call | tf_op jit(solution)/shard_map/pallas_call | solution.py:445

commit v10 on v9

--- a/solution.py
+++ b/solution.py
@@ -18,6 +18,7 @@
 BIG = 2
 SMALL_ROWS = 8
 LAST_ROWS = 4
+STRAIGHT = 1
 SMALLS = 9
 LAG = 6
 EARLY = 3
@@ -172,34 +173,29 @@
         masks.append(jnp.broadcast_to(jnp.where(m > 0, 0.0, -1e9).astype(F32), (width, width)).T)
 
     paired = lax.rem(row + CORES, n_row)
-    hand = remote(bsend, relay, b1_send.at[0], b1_recv.at[0], paired, col)
+    parts = (slice(0, heads), slice(0, STRAIGHT), slice(STRAIGHT, heads))
+    of = lambda ref, t: ref.at[pl.ds(parts[t].start, parts[t].stop - parts[t].start)]
+    tile_of = lambda slot, t: of(btile.at[slot], t)
     cross_slot = (CORES + core) * CORES + jslot
-    cross = remote(relay, btile.at[cross_slot], b1_send.at[1], b1_recv.at[1], row, far + core)
-
-    direct = remote(bsend, btile.at[cross_slot], b1_send.at[1], b1_recv.at[1], row, far + core)
-    detour_out = jnp.logical_or(chip == 1, core == 1)
-    detour_in = jnp.logical_or(chip == 0, core == 1)
+    straight = remote(of(bsend, 1), tile_of(cross_slot, 1), b1_send.at[0], b1_recv.at[0], row, far + core)
+    hand = remote(of(bsend, 2), of(relay, 2), b1_send.at[1], b1_recv.at[1], paired, col)
+    cross = remote(of(relay, 2), tile_of(cross_slot, 2), b1_send.at[2], b1_recv.at[2], row, far + core)
     away = jnp.logical_not(home)
-    lands = jnp.logical_or(jnp.logical_and(detour_in, away), jnp.logical_and(jnp.logical_not(detour_in), home))
-
-    def spread(src, slot, t, d):
-        return remote(src, btile.at[slot], b2_send.at[t, d - 1], b2_recv.at[t, jslot], lax.rem(row + d, n_row), col)
-
-    @pl.when(jnp.logical_and(away, detour_out))
+
+    def spread(t, d):
+        slot = home_slot if t == 0 else cross_slot
+        return remote(bsend if t == 0 else tile_of(slot, t), tile_of(slot, t), b2_send.at[t, d - 1], b2_recv.at[t, jslot],
+                      lax.rem(row + d, n_row), col)
+
+    @pl.when(away)
     def _():
         hand.start()
-
-    @pl.when(jnp.logical_and(away, jnp.logical_not(detour_out)))
-    def _():
-        direct.start()
+        straight.start()
 
     @pl.when(home)
     def _():
         for d in range(1, 4):
-            spread(bsend, home_slot, 0, d).start()
-
-    @pl.when(jnp.logical_and(home, detour_out))
-    def _():
+            spread(0, d).start()
         hand.wait_recv()
         cross.start()
 
@@ -208,11 +204,17 @@
         for k in range(CORES):
             small(g, k, core).start()
 
-    @pl.when(lands)
+    @pl.when(home)
+    def _():
+        straight.wait_recv()
+        for d in range(1, 4):
+            spread(1, d).start()
+
+    @pl.when(away)
     def _():
         cross.wait_recv()
         for d in range(1, 4):
-            spread(btile.at[cross_slot], cross_slot, 1, d).start()
+            spread(2, d).start()
 
     def forward(t, j):
         slot = (core + CORES * t) * CORES + j
@@ -221,13 +223,11 @@
     for t in range(2):
         for j in range(CORES):
             slot = (core + CORES * t) * CORES + j
-            source = chip * CORES + j
-            if t == 1:
-                source = jnp.where(detour_in, far + j, source)
-
-            @pl.when(row != source)
-            def _():
-                remote(bsend, btile.at[slot], b1_send.at[0], b2_recv.at[t, j], row, partner).wait_recv()
+            for part, source in ((0, chip * CORES + j),) if t == 0 else ((1, chip * CORES + j), (2, far + j)):
+
+                @pl.when(row != source)
+                def _():
+                    remote(of(bsend, part), tile_of(slot, part), b1_send.at[0], b2_recv.at[part, j], row, partner).wait_recv()
 
             forward(t, j).start()
     for j in range(CORES):
@@ -373,23 +373,19 @@
         for k in range(CORES):
             small(g, k, core).wait_send()
 
-    @pl.when(jnp.logical_and(away, detour_out))
+    @pl.when(away)
     def _():
         hand.wait_send()
-
-    @pl.when(jnp.logical_or(jnp.logical_and(home, detour_out), jnp.logical_and(away, jnp.logical_not(detour_out))))
+        straight.wait_send()
+        for d in range(1, 4):
+            spread(2, d).wait_send()
+
+    @pl.when(home)
     def _():
         cross.wait_send()
-
-    @pl.when(home)
-    def _():
-        for d in range(1, 4):
-            spread(bsend, home_slot, 0, d).wait_send()
-
-    @pl.when(lands)
-    def _():
-        for d in range(1, 4):
-            spread(btile.at[cross_slot], cross_slot, 1, d).wait_send()
+        for t in range(2):
+            for d in range(1, 4):
+                spread(t, d).wait_send()
 
     for j in range(CORES):
         for t in range(2):
@@ -437,7 +433,7 @@
                 *pairs((n_k, chan), BF16), *pairs((n_k, proj), BF16), *pairs((proj, n_k), BF16),
                 *pairs((proj, n_q), BF16), *pairs((proj, n_q), F32),
                 *[vmem((n_k, n_q), F32)] * 8, *pairs((proj, n_q), BF16),
-                pltpu.SemaphoreType.REGULAR((2,)), dma((len(smalls),)), dma((2,)), dma, dma, dma((CORES, groups)), dma((CORES, groups)), dma((2,)), dma((2,)), dma((2, 3)), dma((2, CORES)),
+                pltpu.SemaphoreType.REGULAR((2,)), dma((len(smalls),)), dma((2,)), dma, dma, dma((CORES, groups)), dma((CORES, groups)), dma((3,)), dma((3,)), dma((3, 3)), dma((3, CORES)),
                 dma((2, CORES)), dma((2, CORES)), dma((groups,)), dma((groups,)),
             ],
             compiler_params=pltpu.CompilerParams(collective_id=0, has_side_effects=True, vmem_limit_bytes=58_000_000),

time: 106 us -> 105 us (level); the launches traced: 104 us -> 105 us
  no operation moved by 1% of the time
where the time goes in v10:
time: 105 us
  Pallas kernels  105 us (100%)
    pallas_call x1, Pallas kernels, per_device(): pl.pallas_call(functools.partial(kernel, heads), in_specs=[hbm] * (1 + le...  103 us

profile of v10, /device:TPU:0, one launch (start us, length us, event | category | flops | bytes accessed | tf_op | source)
XLA Modules:
  0.0 104.6 jit_solution(8504920777150802765)
XLA Ops:
  0.0 102.6 %shard_map.100.src = bf16[128,128,128]{2,1,0:T(8,128)(2,1)S(1)} custom-call(bf16[128,128,128]{2,1,0:T(8,128)(2,1)} %z_hbm.1, s32[1,512]{1,0:T(1,128)} %bitcast.4, f32[1,128]{1,0:T(1,128)} %bitcast.6, f32[1,128]{1,0:T(1,128)} %bitcast.7, bf16[128,128]{1,0:T(8,128)(2,1)} %refs_3_.1, bf16[128,128]{1,0:T(8,128)(2,1)} %refs_4_.1, bf16[128,128]{1,0:T(8,128)(2,1)} %refs_5_.1, ...), custom_call_target="tpu_custom_call" | custom-call | tf_op jit(solution)/shard_map/pallas_call | solution.py:423
  102.6 2.0 %shard_map.101 = bf16[128,128,128]{2,1,0:T(8,128)(2,1)} custom-call(bf16[128,128,128]{2,1,0:T(8,128)(2,1)S(1)} %shard_map.100.src), custom_call_target="tpu_custom_call" | custom-call | tf_op jit(solution)/shard_map/pallas_call | solution.py:441

commit v11 on v10

--- a/solution.py
+++ b/solution.py
@@ -44,7 +44,7 @@
 
 def body(heads, z_hbm, small_hbm, small_refs, out_ref,
            wt_ref, zbuf, own, outv, bias, btile, bsend, relay, brow, a0, a1, k0, k1, v0, v1, q0, q1, g0, g1,
-           s0, s1, s2, s3, s4, s5, s6, s7, go0, go1,
+           s0, s1, s2, s3, s4, s5, s6, s7, go0, go1, st0, st1, pa0, pa1,
            round_sem, small_sem, local_sem, zp_send, zp_recv, zs_send, zs_recv, b1_send, b1_recv, b2_send, b2_recv,
            b3_send, b3_recv, o_send, o_recv):
     mask_ref, gamma_ref, beta_ref, wq_ref, wk_ref, wv_ref, wbt_ref, wg_ref, wo_ref = small_refs
@@ -242,7 +242,7 @@
                 bias[h, s * width:(s + 1) * width, j * width:(j + 1) * width] = (b + masks[s]) * LOG2E
 
     a_s, k_s, v_s, q_s, g_s = (a0, a1), (k0, k1), (v0, v1), (q0, q1), (g0, g1)
-    sc, go = ((s0, s1, s2, s3), (s4, s5, s6, s7)), (go0, go1)
+    sc, go, stats, partial = ((s0, s1, s2, s3), (s4, s5, s6, s7)), (go0, go1), (st0, st1), (pa0, pa1)
     scale = hd ** -0.5 * LOG2E
 
     every, near, distant = slice(0, 2 * n_q), slice(0, n_q), slice(n_q, 2 * n_q)
@@ -298,6 +298,30 @@
         remote(outv.at[pl.ds(0, STEP_ROWS)], out_ref.at[pl.ds((1 - core) * rows + g * STEP_ROWS, STEP_ROWS)],
                o_send.at[g], o_recv.at[g], row, partner).wait_recv()
         return carry
+
+    def weigh(h, slot, keys, top):
+        s = sc[slot][h][keys, :]
+        m = over_keys(s, jnp.max)
+        if top is not None:
+            m = jnp.maximum(m, top)
+        p = jnp.exp2(s - m)
+        at = slice(h * hd, (h + 1) * hd)
+        return m, over_keys(p, jnp.sum), jnp.dot(v_s[slot][at, keys], p.astype(BF16), preferred_element_type=F32)
+
+    def attend_near(h, slot):
+        m, total, o = weigh(h, slot, near, None)
+        stats[slot][h:h + 1, :] = m
+        stats[slot][heads + h:heads + h + 1, :] = total
+        partial[slot][h * hd:(h + 1) * hd, :] = o
+
+    def attend_distant(h, slot, dst):
+        top = stats[slot][h:h + 1, :]
+        m, total, o = weigh(h, slot, distant, top)
+        rescale = jnp.exp2(top - m)
+        at = slice(h * hd, (h + 1) * hd)
+        o = partial[slot][at, :] * rescale + o
+        total = stats[slot][heads + h:heads + h + 1, :] * rescale + total
+        dst[at, :] = (g_s[slot][at, :] * (o / total)).astype(BF16)
 
     def step(i, carry):
         @pl.when(i < steps)
@@ -338,14 +362,18 @@
             queries_of(r)
             gates_of(r)
             values_of(r, near)
-        for r, h in units:
+        ahead = 2
+        for r, h in units[:ahead]:
             scores(r, h, sc[r], near)
+        for n, (r, h) in enumerate(units):
+            for r2, h2 in units[n + ahead:n + ahead + 1]:
+                scores(r2, h2, sc[r2], near)
+            attend_near(h, r)
         z_wait(i)
         for r in both:
             norm(i * STEP_ROWS + r, r, distant)
         for r in both:
             keys_of(r, distant)
-        ahead = 2
         for r, h in units[:ahead]:
             scores(r, h, sc[r], distant)
         for r in both:
@@ -353,7 +381,7 @@
         for n, (r, h) in enumerate(units):
             for r2, h2 in units[n + ahead:n + ahead + 1]:
                 scores(r2, h2, sc[r2], distant)
-            attend(h, r, sc[r], go[r])
+            attend_distant(h, r, go[r])
         for r in both:
             finish(i * STEP_ROWS + r, go[r])
         return carry
@@ -433,6 +461,7 @@
                 *pairs((n_k, chan), BF16), *pairs((n_k, proj), BF16), *pairs((proj, n_k), BF16),
                 *pairs((proj, n_q), BF16), *pairs((proj, n_q), F32),
                 *[vmem((n_k, n_q), F32)] * 8, *pairs((proj, n_q), BF16),
+                *pairs((2 * heads, n_q), F32), *pairs((proj, n_q), F32),
                 pltpu.SemaphoreType.REGULAR((2,)), dma((len(smalls),)), dma((2,)), dma, dma, dma((CORES, groups)), dma((CORES, groups)), dma((3,)), dma((3,)), dma((3, 3)), dma((3, CORES)),
                 dma((2, CORES)), dma((2, CORES)), dma((groups,)), dma((groups,)),
             ],

time: 105 us -> 106 us (level)
  no operation moved by 1% of the time
where the time goes in v11:
time: 106 us; the launch traced here: 105 us
  Pallas kernels  105 us (99%)
    pallas_call x1, Pallas kernels, per_device(): pl.pallas_call(functools.partial(kernel, heads), in_specs=[hbm] * (1 + le...  103 us

profile of v11, /device:TPU:0, one launch (start us, length us, event | category | flops | bytes accessed | tf_op | source)
XLA Modules:
  0.0 105.3 jit_solution(16627388492532814382)
XLA Ops:
  0.0 103.3 %shard_map.100.src = bf16[128,128,128]{2,1,0:T(8,128)(2,1)S(1)} custom-call(bf16[128,128,128]{2,1,0:T(8,128)(2,1)} %z_hbm.1, s32[1,512]{1,0:T(1,128)} %bitcast.4, f32[1,128]{1,0:T(1,128)} %bitcast.6, f32[1,128]{1,0:T(1,128)} %bitcast.7, bf16[128,128]{1,0:T(8,128)(2,1)} %refs_3_.1, bf16[128,128]{1,0:T(8,128)(2,1)} %refs_4_.1, bf16[128,128]{1,0:T(8,128)(2,1)} %refs_5_.1, ...), custom_call_target="tpu_custom_call" | custom-call | tf_op jit(solution)/shard_map/pallas_call | solution.py:451
  103.3 2.0 %shard_map.101 = bf16[128,128,128]{2,1,0:T(8,128)(2,1)} custom-call(bf16[128,128,128]{2,1,0:T(8,128)(2,1)S(1)} %shard_map.100.src), custom_call_target="tpu_custom_call" | custom-call | tf_op jit(solution)/shard_map/pallas_call | solution.py:470

commit v12 on v10

--- a/solution.py
+++ b/solution.py
@@ -17,10 +17,12 @@
 STEP_ROWS = 2
 BIG = 2
 SMALL_ROWS = 8
-LAST_ROWS = 4
+LAST_ROWS = 8
 STRAIGHT = 1
 SMALLS = 9
-LAG = 6
+SETTLE = 26
+SETTLED_Z = 11
+SETTLED_OUT = 22
 EARLY = 3
 
 
@@ -300,6 +302,11 @@
         return carry
 
     def step(i, carry):
+        @pl.when(i == SETTLE)
+        def _():
+            lax.fori_loop(0, SETTLED_Z, sent, 0)
+            lax.fori_loop(0, SETTLED_OUT, drained, 0)
+
         @pl.when(i < steps)
         def _():
             z_wait(i)
@@ -363,12 +370,10 @@
     lax.fori_loop(0, steps + 1, step, 0)
     finish(steps * STEP_ROWS - 1, go[0])
     out_copy(steps - 2).start()
-    lax.fori_loop(0, bigs - LAG, sent, 0)
-    lax.fori_loop(0, steps + 1 - LAG, drained, 0)
     lax.fori_loop(steps, groups, last_rows, 0)
     to_partner.wait_send()
     out_copy(groups - 1).start()
-    lax.fori_loop(bigs - LAG, bigs, sent, 0)
+    lax.fori_loop(SETTLED_Z, bigs, sent, 0)
     for g in range(bigs * BIG, groups):
         for k in range(CORES):
             small(g, k, core).wait_send()
@@ -391,7 +396,7 @@
         for t in range(2):
             forward(t, j).wait_send()
 
-    lax.fori_loop(steps + 1 - LAG, groups, drained, 0)
+    lax.fori_loop(SETTLED_OUT, groups, drained, 0)
 
 
 def write_out(src, dst, sem):

time: 105 us -> 106 us (level)
  no operation moved by 1% of the time
where the time goes in v12:
time: 106 us
  Pallas kernels  105 us (99%)
    pallas_call x1, Pallas kernels, per_device(): pl.pallas_call(functools.partial(kernel, heads), in_specs=[hbm] * (1 + le...  103 us

profile of v12, /device:TPU:0, one launch (start us, length us, event | category | flops | bytes accessed | tf_op | source)
XLA Modules:
  0.0 105.5 jit_solution(11832046569845240787)
XLA Ops:
  0.0 103.5 %shard_map.100.src = bf16[128,128,128]{2,1,0:T(8,128)(2,1)S(1)} custom-call(bf16[128,128,128]{2,1,0:T(8,128)(2,1)} %z_hbm.1, s32[1,512]{1,0:T(1,128)} %bitcast.4, f32[1,128]{1,0:T(1,128)} %bitcast.6, f32[1,128]{1,0:T(1,128)} %bitcast.7, bf16[128,128]{1,0:T(8,128)(2,1)} %refs_3_.1, bf16[128,128]{1,0:T(8,128)(2,1)} %refs_4_.1, bf16[128,128]{1,0:T(8,128)(2,1)} %refs_5_.1, ...), custom_call_target="tpu_custom_call" | custom-call | tf_op jit(solution)/shard_map/pallas_call | solution.py:428
  103.5 2.0 %shard_map.101 = bf16[128,128,128]{2,1,0:T(8,128)(2,1)} custom-call(bf16[128,128,128]{2,1,0:T(8,128)(2,1)S(1)} %shard_map.100.src), custom_call_target="tpu_custom_call" | custom-call | tf_op jit(solution)/shard_map/pallas_call | solution.py:446

commit v13 on v10

--- a/solution.py
+++ b/solution.py
@@ -17,10 +17,9 @@
 STEP_ROWS = 2
 BIG = 2
 SMALL_ROWS = 8
-LAST_ROWS = 4
+LAST_ROWS = 2
 STRAIGHT = 1
 SMALLS = 9
-LAG = 6
 EARLY = 3
 
 
@@ -363,12 +362,10 @@
     lax.fori_loop(0, steps + 1, step, 0)
     finish(steps * STEP_ROWS - 1, go[0])
     out_copy(steps - 2).start()
-    lax.fori_loop(0, bigs - LAG, sent, 0)
-    lax.fori_loop(0, steps + 1 - LAG, drained, 0)
     lax.fori_loop(steps, groups, last_rows, 0)
     to_partner.wait_send()
     out_copy(groups - 1).start()
-    lax.fori_loop(bigs - LAG, bigs, sent, 0)
+    lax.fori_loop(0, bigs, sent, 0)
     for g in range(bigs * BIG, groups):
         for k in range(CORES):
             small(g, k, core).wait_send()
@@ -391,7 +388,7 @@
         for t in range(2):
             forward(t, j).wait_send()
 
-    lax.fori_loop(steps + 1 - LAG, groups, drained, 0)
+    lax.fori_loop(0, groups, drained, 0)
 
 
 def write_out(src, dst, sem):

time: 105 us -> 105 us (level)
  no operation moved by 1% of the time
where the time goes in v13:
time: 105 us
  Pallas kernels  105 us (100%)
    pallas_call x1, Pallas kernels, per_device(): pl.pallas_call(functools.partial(kernel, heads), in_specs=[hbm] * (1 + le...  103 us

profile of v13, /device:TPU:0, one launch (start us, length us, event | category | flops | bytes accessed | tf_op | source)
XLA Modules:
  0.0 104.7 jit_solution(5574891122827170135)
XLA Ops:
  0.0 102.7 %shard_map.100.src = bf16[128,128,128]{2,1,0:T(8,128)(2,1)S(1)} custom-call(bf16[128,128,128]{2,1,0:T(8,128)(2,1)} %z_hbm.1, s32[1,512]{1,0:T(1,128)} %bitcast.4, f32[1,128]{1,0:T(1,128)} %bitcast.6, f32[1,128]{1,0:T(1,128)} %bitcast.7, bf16[128,128]{1,0:T(8,128)(2,1)} %refs_3_.1, bf16[128,128]{1,0:T(8,128)(2,1)} %refs_4_.1, bf16[128,128]{1,0:T(8,128)(2,1)} %refs_5_.1, ...), custom_call_target="tpu_custom_call" | custom-call | tf_op jit(solution)/shard_map/pallas_call | solution.py:420
  102.7 2.0 %shard_map.101 = bf16[128,128,128]{2,1,0:T(8,128)(2,1)} custom-call(bf16[128,128,128]{2,1,0:T(8,128)(2,1)S(1)} %shard_map.100.src), custom_call_target="tpu_custom_call" | custom-call | tf_op jit(solution)/shard_map/pallas_call | solution.py:438

commit v14 on v12

--- a/solution.py
+++ b/solution.py
@@ -17,12 +17,12 @@
 STEP_ROWS = 2
 BIG = 2
 SMALL_ROWS = 8
-LAST_ROWS = 8
+LAST_ROWS = 4
 STRAIGHT = 1
 SMALLS = 9
-SETTLE = 26
-SETTLED_Z = 11
-SETTLED_OUT = 22
+SETTLE = 29
+SETTLED_Z = 12
+SETTLED_OUT = 24
 EARLY = 3
 
 

time: 106 us -> 105 us (level)
    pallas_call x1, Pallas kernels: 103 us -> 102 us  [per_device(): pl.pallas_call(functools.partial(kernel, heads), in_specs=[hbm] * (1 + le...]
where the time goes in v14:
time: 105 us; the launch traced here: 104 us
  Pallas kernels  104 us (99%)
    pallas_call x1, Pallas kernels, per_device(): pl.pallas_call(functools.partial(kernel, heads), in_specs=[hbm] * (1 + le...  102 us

profile of v14, /device:TPU:0, one launch (start us, length us, event | category | flops | bytes accessed | tf_op | source)
XLA Modules:
  0.0 104.4 jit_solution(14480546256466391270)
XLA Ops:
  0.0 102.3 %shard_map.100.src = bf16[128,128,128]{2,1,0:T(8,128)(2,1)S(1)} custom-call(bf16[128,128,128]{2,1,0:T(8,128)(2,1)} %z_hbm.1, s32[1,512]{1,0:T(1,128)} %bitcast.4, f32[1,128]{1,0:T(1,128)} %bitcast.6, f32[1,128]{1,0:T(1,128)} %bitcast.7, bf16[128,128]{1,0:T(8,128)(2,1)} %refs_3_.1, bf16[128,128]{1,0:T(8,128)(2,1)} %refs_4_.1, bf16[128,128]{1,0:T(8,128)(2,1)} %refs_5_.1, ...), custom_call_target="tpu_custom_call" | custom-call | tf_op jit(solution)/shard_map/pallas_call | solution.py:428
  102.3 2.0 %shard_map.101 = bf16[128,128,128]{2,1,0:T(8,128)(2,1)} custom-call(bf16[128,128,128]{2,1,0:T(8,128)(2,1)S(1)} %shard_map.100.src), custom_call_target="tpu_custom_call" | custom-call | tf_op jit(solution)/shard_map/pallas_call | solution.py:446
